TPU v7x, 32 devices: a whole 2x2x4 slice. The times are simulated.
32 devices in a mesh: dp: 2 (over x), tp: 4 (over z), sp: 4 (over y, core).
Axes of the slice: x: 2, y: 2, z: 4, core: 2. Of those that a mesh axis runs over, the one named last changes fastest.
Arguments:
- hidden: bfloat16 [2048, 2048], P('dp'), parts along dimension 0
- start_pos: int32 [2], P('dp'), parts along dimension 0
- k_cache: bfloat16 [32768, 8, 128], P(('dp', 'sp'), 'tp'), parts along dimension 0
- v_cache: bfloat16 [32768, 8, 128], P(('dp', 'sp'), 'tp'), parts along dimension 0
- norm_gain: float32 [2048], replicated
- w_query: bfloat16 [2048, 2048], P(None, 'tp')
- w_key: bfloat16 [2048, 1024], P(None, 'tp')
- w_value: bfloat16 [2048, 1024], P(None, 'tp')
- q_gain: float32 [128], replicated
- k_gain: float32 [128], replicated
- w_out: bfloat16 [2048, 2048], P('tp')
Outputs:
- output 1: bfloat16 [2048, 2048], P('dp'), parts along dimension 0
- output 2: bfloat16 [32768, 8, 128], P(('dp', 'sp'), 'tp'), parts along dimension 0
- output 3: bfloat16 [32768, 8, 128], P(('dp', 'sp'), 'tp'), parts along dimension 0
There are 2 independent parts. A program takes and returns all parts, laid end to end along the dimension named above; an argument that names none is the same for every part.
All inputs are finite; a program needn't handle non-finite values.
Results may differ from a plain program's by a relative error of at most 0.0042618.
Values sent between devices are 32-bit elements.
A program may use at most 1 GiB of HBM per device.

v0:
```python
import jax
import jax.numpy as jnp
from jax import lax
from jax.sharding import PartitionSpec as P

ROPE_BASE = 1e6
NORM_EPS = 1e-6


def rms_norm(values, gain):
    mean_sq = jnp.mean(values * values, axis=-1, keepdims=True)
    return values * lax.rsqrt(mean_sq + NORM_EPS) * gain


def rotary(values, positions):
    half_dim = values.shape[-1] // 2
    inv_freq = ROPE_BASE ** (-2.0 * jnp.arange(half_dim, dtype=jnp.float32) / values.shape[-1])
    angles = positions.astype(jnp.float32)[:, None] * inv_freq[None, :]
    angles = angles.reshape((positions.shape[0],) + (1,) * (values.ndim - 2) + (half_dim,))
    cosine = jnp.cos(angles)
    sine = jnp.sin(angles)
    x_first = values[..., :half_dim]
    x_second = values[..., half_dim:]
    return jnp.concatenate([x_first * cosine - x_second * sine, x_second * cosine + x_first * sine], axis=-1)


def write_rows(shard, new_rows, write_at):
    chunk_len = new_rows.shape[0]
    shard_len = shard.shape[0]
    zero_rows = jnp.zeros((chunk_len,) + shard.shape[1:], shard.dtype)
    extended = jnp.concatenate([zero_rows, shard, zero_rows], axis=0)
    extended = lax.dynamic_update_slice(extended, new_rows, (write_at, 0, 0))
    return extended[chunk_len:chunk_len + shard_len]


def solution(mesh):
    cache_spec = P(("dp", "sp"), "tp", None)
    in_specs = (P("dp", None), P("dp"), cache_spec, cache_spec, P(None), P(None, "tp"), P(None, "tp"), P(None, "tp"), P(None), P(None), P("tp", None))
    out_specs = (P("dp", None), cache_spec, cache_spec)

    def local_step(hidden, start_pos, k_shard, v_shard, norm_gain, w_query, w_key, w_value, q_gain, k_gain, w_out):
        chunk_len, model_dim = hidden.shape
        shard_len, kv_local, head_dim = k_shard.shape
        group_size = w_query.shape[1] // head_dim // kv_local
        first_pos = start_pos[0]
        positions = first_pos + jnp.arange(chunk_len, dtype=jnp.int32)
        normed = rms_norm(hidden.astype(jnp.float32), norm_gain).astype(jnp.bfloat16)
        q_proj = jnp.dot(normed, w_query, preferred_element_type=jnp.float32).reshape(chunk_len, kv_local, group_size, head_dim)
        k_proj = jnp.dot(normed, w_key, preferred_element_type=jnp.float32).reshape(chunk_len, kv_local, head_dim)
        v_new = jnp.dot(normed, w_value, preferred_element_type=jnp.float32).reshape(chunk_len, kv_local, head_dim).astype(jnp.bfloat16)
        q_rot = rotary(rms_norm(q_proj, q_gain), positions).astype(jnp.bfloat16)
        k_rot = rotary(rms_norm(k_proj, k_gain), positions).astype(jnp.bfloat16)
        shard_first = lax.axis_index("sp") * shard_len
        write_at = jnp.clip(first_pos - shard_first + chunk_len, 0, shard_len + chunk_len)
        k_upd = write_rows(k_shard, k_rot, write_at)
        v_upd = write_rows(v_shard, v_new, write_at)
        key_pos = shard_first + jnp.arange(shard_len, dtype=jnp.int32)
        allowed = (key_pos[None, :] <= positions[:, None])[None, :, None, :]
        scores = jnp.einsum("cngd,tnd->ncgt", q_rot, k_upd, preferred_element_type=jnp.float32) * (head_dim ** -0.5)
        scores = jnp.where(allowed, scores, -jnp.inf)
        global_max = lax.pmax(jnp.max(scores, axis=-1), "sp")
        weights = jnp.exp(scores - global_max[..., None])
        numerator = jnp.einsum("ncgt,tnd->ncgd", weights.astype(jnp.bfloat16), v_upd, preferred_element_type=jnp.float32)
        denominator = jnp.sum(weights, axis=-1)
        numerator = lax.psum(numerator, "sp")
        denominator = lax.psum(denominator, "sp")
        attention = (numerator / denominator[..., None]).astype(jnp.bfloat16)
        w_heads = w_out.reshape(kv_local, group_size, head_dim, model_dim)
        head_sum = jnp.einsum("ncgd,ngde->ce", attention, w_heads, preferred_element_type=jnp.float32)
        head_sum = lax.psum(head_sum, "tp")
        out = (hidden.astype(jnp.float32) + head_sum).astype(jnp.bfloat16)
        return out, k_upd, v_upd

    return jax.shard_map(local_step, mesh=mesh, in_specs=in_specs, out_specs=out_specs, check_vma=False)
```

profile of v0, /device:TPU:0, one launch (start us, length us, event | category | flops | bytes accessed | tf_op | source)
XLA Modules:
  0.0 543.6 jit_solution(6427819620497658982)
XLA Ops:
  7.3 3.2 fusion.5
  10.8 3.7 multiply_reduce_fusion.1
  16.8 3.3 copy.23
  20.1 5.5 %multiply_reduce_fusion = (f32[1024,2,2]{0,2,1:T(2,128)S(1)}, f32[1024,512]{0,1:T(8,128)}) fusion(bf16[2048,512]{1,0:T(8,128)(2,1)} %param.16, bf16[1024,2048]{1,0:T(8,128)(2,1)S(1)} %copy-done.4, f32[2048]{0:T(1024)S(1)} %copy-done.8, f32[1024]{0:T(1024)S(1)} %add_rsqrt_fusion.2), kind=kOutput, calls=%fused_computation.26 | convolution fusion | flops 2156916736 | bytes 8417280 | tf_op jit(solution)/shard_map/dot_general | solution.py:48
  25.6 3.1 copy.22
  32.9 2.1 subtract_convert_fusion
  35.4 3.0 pad_maximum_fusion
  38.3 4.7 broadcast_compare_fusion
  43.1 3.5 dynamic_update_slice.6
  46.6 27.3 %fusion = (f32[2,1024,2]{1,2,0:T(2,128)S(1)}, f32[2,1024,2,4096]{3,1,2,0:T(8,128)}) fusion(pred[1024,4096]{1,0:T(8,128)(4,1)} %broadcast_compare_fusion, bf16[6144,2,128]{2,0,1:T(8,128)(2,1)} %dynamic_update_slice.6, bf16[1024,2,2,64]{3,0,2,1:T(8,128)(2,1)} %get-tuple-element.12, bf16[1024,2,2,64]{3,0,2,1:T(8,128)(2,1)} %get-tuple-element.11), kind=kOutput, calls=%fused_computation.2 | convolution fusion | flops 4347392000 | bytes 75513856 | tf_op jit(solution)/shard_map/cngd,tnd->ncgt/dot_general | solution.py:59
  73.9 13.7 %pmax.7 = f32[2,1024,2]{1,2,0:T(2,128)S(1)} all-reduce(f32[2,1024,2]{1,2,0:T(2,128)S(1)} %get-tuple-element.21), channel_id=1, replica_groups=mesh['dp'=2,'tp'=4,'sp'=4] {'sp'}, use_global_device_ids=true, to_apply=%region_4.5 | all-reduce | flops 4096 | bytes 32768 | tf_op jit(solution)/shard_map/pmax | solution.py:61
  87.6 4.0 convolution_convert_fusion
  92.3 32.6 %pad_maximum_fusion.1 = bf16[6144,2,128]{2,1,0:T(2,128)(2,1)S(1)} fusion(bf16[1024,2,128]{2,1,0:T(2,128)(2,1)S(1)} %broadcast.149.clone, bf16[4096,2,128]{2,1,0:T(2,128)(2,1)} %param.14), kind=kLoop, calls=%fused_computation.17 | loop fusion | flops 3145728 | bytes 5767168 | tf_op jit(solution)/shard_map/concatenate | solution.py:31
  126.9 2.7 slice_bitcast_fusion
  129.6 34.7 %fusion.1 = (f32[2,1024,2]{1,2,0:T(2,128)S(1)}, bf16[2,1024,2,4096]{3,1,2,0:T(8,128)(2,1)}) fusion(f32[2,1024,2,4096]{3,1,2,0:T(8,128)} %get-tuple-element.22, f32[2,1024,2]{1,2,0:T(2,128)S(1)} %pmax.7, pred[1024,4096]{1,0:T(8,128)(4,1)} %broadcast_compare_fusion), kind=kLoop, calls=%fused_computation.3 | loop fusion | flops 83881984 | bytes 104890368 | tf_op jit(solution)/shard_map/reduce_sum | solution.py:64
  164.2 16.9 %fusion.3 = f32[2,1024,2,128]{3,1,0,2:T(8,128)} fusion(bf16[2,1024,2,4096]{3,1,2,0:T(8,128)(2,1)} %get-tuple-element.10, bf16[4096,2,128,1]{2,1,0,3:T(2,128)(2,1)} %slice_bitcast_fusion), kind=kOutput, calls=%fused_computation.5 | convolution fusion | flops 4294967296 | bytes 37748736 | tf_op jit(solution)/shard_map/ncgt,tnd->ncgd/dot_general | solution.py:63
  181.2 10.7 %psum.22 = f32[2,1024,2]{1,2,0:T(2,128)S(1)} all-reduce(f32[2,1024,2]{1,2,0:T(2,128)S(1)} %get-tuple-element.9), channel_id=1, replica_groups=mesh['dp'=2,'tp'=4,'sp'=4] {'sp'}, use_global_device_ids=true, to_apply=%region_7.8 | all-reduce | flops 4096 | bytes 32768 | tf_op jit(solution)/shard_map/psum | solution.py:66
  191.9 41.0 %all-reduce.3.cloned.1.call-done = f32[2,1024,2,128]{3,1,0,2:T(8,128)} async-done(((f32[2,1024,2,128]{3,1,0,2:T(8,128)}), f32[2,1024,2,128]{3,1,0,2:T(8,128)}) %all-reduce.3.cloned.1.call-update) | async-done | bytes 2097168 | tf_op jit(solution)/shard_map/psum | solution.py:65
  232.9 6.2 %convolution_bitcast_fusion = f32[1024,2048]{1,0:T(8,128)} fusion(bf16[2,2,128,2048]{3,2,1,0:T(8,128)(2,1)S(1)} %bitcast.25, f32[2,1024,2,128]{3,1,0,2:T(8,128)} %all-reduce.3.cloned.1.call-done, f32[2,1024,2]{1,0,2:T(2,128)S(1)} %copy.28), kind=kOutput, calls=%fused_computation.15 | convolution fusion | flops 2148532224 | bytes 12599296 | tf_op jit(solution)/shard_map/ncgd,ngde->ce/dot_general | solution.py:69
  239.1 1.9 slice.28
  241.6 2.7 slice.29
  244.3 18.1 %copy.30 = bf16[4096,2,128]{2,1,0:T(2,128)(2,1)} copy(bf16[4096,2,128]{2,0,1:T(8,128)(2,1)S(1)} %slice.28) | data formatting | bytes 4194304
  262.4 265.7 %all-reduce.5.cloned.1.call-done = f32[1024,2048]{1,0:T(8,128)} async-done(((f32[1024,2048]{1,0:T(8,128)}), f32[1024,2048]{1,0:T(8,128)}) %all-reduce.5.cloned.1.call-update) | async-done | bytes 8388624 | tf_op jit(solution)/shard_map/psum | solution.py:70
  528.1 8.3 %fusion.8 = bf16[1024,2048]{1,0:T(8,128)(2,1)} fusion(f32[1024,2048]{1,0:T(8,128)} %all-reduce.5.cloned.1.call-done, bf16[1024,2048]{1,0:T(8,128)(2,1)} %param.11), kind=kLoop, calls=%fused_computation.13 | loop fusion | flops 6291456 | bytes 16777216 | tf_op jit(solution)/shard_map/convert_element_type | solution.py:71
  (39 shorter events, 9.9 us)
Async XLA Ops:
  7.2 225.7 %copy-start = (bf16[512,2048]{1,0:T(8,128)(2,1)S(1)}, bf16[512,2048]{1,0:T(8,128)(2,1)}, u32[]{:S(2)}) copy-start(bf16[512,2048]{1,0:T(8,128)(2,1)} %param.21) | copy-start | bytes 6291460
  7.2 3.3 copy-start.8
  7.2 225.7 %all-reduce.3.cloned.1.call-start = ((), (), s32[]{:S(2)}) async-start(), calls=%async_computation | async-start | bytes 4194304 | tf_op jit(solution)/shard_map/psum | solution.py:65
  7.2 3.6 copy-start.3
  16.8 3.3 copy-start.4
  25.6 5.0 copy-start.6
  30.6 1.6 copy-start.5
  30.6 1.6 copy-start.7
  125.3 1.6 copy-start.1
  181.1 346.9 %all-reduce.5.cloned.1.call-start = ((), (), s32[]{:S(2)}) async-start(), calls=%async_computation.1 | async-start | bytes 16777216 | tf_op jit(solution)/shard_map/psum | solution.py:70
  239.1 2.5 copy-start.2
Sparse Core Ops, SparseCore 0:
  181.2 51.5 all-reduce.2
  239.2 288.8 all-reduce.4
where the time goes:
time: 548 us; the launch traced here: 544 us
  waiting for transfers between devices  307 us (56%)
  other arithmetic  92.2 us (17%)
  matrix products  63.6 us (12%)
  local copies, waits for them, and re-layouts  41.3 us (8%)
  blocking collectives  24.4 us (4%)
  between operations  15.3 us (3%)
    psum x1, waiting for transfers between devices, local_step(): head_sum = lax.psum(head_sum, 'tp')  266 us
    psum x1, waiting for transfers between devices, local_step(): numerator = lax.psum(numerator, 'sp')  41 us
    concatenate x2, other arithmetic, write_rows(): extended = jnp.concatenate([zero_rows, shard, zero_rows], axis=0)  35.5 us
    reduce_sum x1, other arithmetic, local_step(): denominator = jnp.sum(weights, axis=-1)  34.7 us
    dot_general x1, matrix products, local_step(): jnp.einsum('cngd,tnd->ncgt', q_rot, k_upd, preferred_element_type=jnp.flo...  27.3 us
    unnamed x20, local copies, waits for them, and re-layouts  24.7 us
    dot_general x1, matrix products, local_step(): jnp.einsum('ncgt,tnd->ncgd', weights.astype(jnp.bfloat16), v_upd, preferr...  16.9 us
    pmax x1, blocking collectives, local_step(): global_max = lax.pmax(jnp.max(scores, axis=-1), 'sp')  13.7 us
  transfers between devices with their start and end apart: 2, of which 2 were waited for; matrix products, arithmetic and copies ran while one was open for 4% of the time, Pallas kernels for 0%

commit v1 on v0

v1 whole, which is shorter than its diff:
```python
import functools

import jax
import jax.numpy as jnp
from jax import lax
from jax.experimental import pallas as pl
from jax.experimental.pallas import tpu as pltpu
from jax.sharding import PartitionSpec as P

ROPE_BASE = 1e6
NORM_EPS = 1e-6
LOG2E = 1.4426950408889634
MESH = pl.DeviceIdType.MESH
F32 = jnp.float32
BF16 = jnp.bfloat16
ROW_BLOCK = 128
STAT_ROWS = 8


def rms_norm(values, gain):
    mean_sq = jnp.mean(values * values, axis=-1, keepdims=True)
    return values * lax.rsqrt(mean_sq + NORM_EPS) * gain


def rotary(values, positions):
    half_dim = values.shape[-1] // 2
    inv_freq = ROPE_BASE ** (-2.0 * jnp.arange(half_dim, dtype=jnp.float32) / values.shape[-1])
    angles = positions.astype(jnp.float32)[:, None] * inv_freq[None, :]
    angles = angles.reshape((positions.shape[0],) + (1,) * (values.ndim - 2) + (half_dim,))
    cosine = jnp.cos(angles)
    sine = jnp.sin(angles)
    x_first = values[..., :half_dim]
    x_second = values[..., half_dim:]
    return jnp.concatenate([x_first * cosine - x_second * sine, x_second * cosine + x_first * sine], axis=-1)


def stats_tile(rows, columns):
    lane = lax.broadcasted_iota(jnp.int32, (rows, 128), 1)
    tile = jnp.zeros((rows, 128), F32)
    for k, column in enumerate(columns):
        tile = jnp.where(lane == k, column, tile)
    return tile


def stats_rows(tile):
    return jnp.transpose(tile)[:STAT_ROWS]


def stats_columns(rows8):
    return jnp.transpose(jnp.concatenate([rows8] * (128 // STAT_ROWS), axis=0))


def merge(num_a, tile_a, num_b, tile_b, scale):
    nums, columns = [], []
    for g in range(2):
        m_a, l_a = tile_a[:, 2 * g:2 * g + 1], tile_a[:, 2 * g + 1:2 * g + 2]
        m_b, l_b = tile_b[:, 2 * g:2 * g + 1], tile_b[:, 2 * g + 1:2 * g + 2]
        m = jnp.maximum(m_a, m_b)
        c_a = jnp.exp2((m_a - m) * scale)
        c_b = jnp.exp2((m_b - m) * scale)
        nums.append(num_a[:, g * 128:(g + 1) * 128] * c_a + num_b[:, g * 128:(g + 1) * 128] * c_b)
        columns += [m, l_a * c_a + l_b * c_b]
    return nums, columns


def attend_kernel(cfg, q_ref, k_ref, v_ref, bias_ref, h_ref, w_ref, out_ref, a_send, a_recv, own_num, own_st, comb_num, comb_st, y_send, y_recv,
                  y_num, y_st, o_own, o_send, o_recv, p_buf, p_recv, m_send, m_recv, f_buf, yf_recv, d1_recv, d2_recv, send_sems, recv_sems):
    nb, rb, keys, chunk_keys, chunk_len, scale, z_count = cfg
    hb = rb // 2
    dp, z, sp = lax.axis_index("dp"), lax.axis_index("tp"), lax.axis_index("sp")
    y, c = lax.div(sp, 2), lax.rem(sp, 2)
    other_y, other_c = 1 - y, 1 - c
    pair_z = z + 1 - 2 * lax.rem(z, 2)
    cross_z = z_count - 1 - z
    is_mid = jnp.logical_and(z >= 1, z <= 2)
    is_end = jnp.logical_not(is_mid)
    half_cols = w_ref.shape[1] // 2
    head_cols = w_ref.shape[0] // 2
    core_peer = (dp, z, y * 2 + other_c)
    y_peer = (dp, z, other_y * 2 + c)
    pair_peer = (dp, pair_z, sp)
    cross_peer = (dp, cross_z, sp)
    my_cols = pl.ds(pl.multiple_of(c * half_cols, half_cols), half_cols)
    peer_cols = pl.ds(pl.multiple_of(other_c * half_cols, half_cols), half_cols)

    barrier = pltpu.get_barrier_semaphore()
    for peer in (core_peer, y_peer, pair_peer):
        pl.semaphore_signal(barrier, inc=1, device_id=peer, device_id_type=MESH)

    @pl.when(is_mid)
    def _():
        pl.semaphore_signal(barrier, inc=1, device_id=cross_peer, device_id_type=MESH)
        pl.semaphore_wait(barrier, 4)

    @pl.when(is_end)
    def _():
        pl.semaphore_wait(barrier, 3)

    def copy(kind, b, src, dst, peer):
        return pltpu.make_async_remote_copy(src.at[b], dst.at[b], send_sems.at[kind, b], recv_sems.at[kind, b], device_id=peer, device_id_type=MESH)

    copy_a = lambda b: copy(0, b, a_send, a_recv, core_peer)
    copy_y = lambda b: copy(1, b, y_send, y_recv, y_peer)
    copy_o = lambda b: copy(2, b, o_send, o_recv, core_peer)
    copy_p = lambda b: copy(3, b, p_buf, p_recv, pair_peer)
    copy_m = lambda b: copy(4, b, m_send, m_recv, cross_peer)
    copy_f = lambda b: copy(5, b, f_buf, f_buf, pair_peer)
    copy_yf = lambda b: copy(6, b, f_buf, yf_recv, y_peer)
    copy_d1 = lambda b: copy(7, b, f_buf, d1_recv, core_peer)
    copy_d2 = lambda b: copy(8, b, yf_recv, d2_recv, core_peer)

    def half_rows(b, which):
        return pl.ds(pl.multiple_of(b * rb + which * hb, hb), hb)

    def attend(b, n):
        q = q_ref[n, b]
        m = l = acc = None
        row = b * rb + lax.rem(lax.broadcasted_iota(jnp.int32, (2 * rb, 1), 0), rb) + jnp.where(sp == 3, 0, keys)
        for start in range(0, keys, chunk_keys):
            s = lax.dot_general(q, k_ref[n, start:start + chunk_keys, :], (((1,), (1,)), ((), ())), preferred_element_type=F32)
            if start >= keys - chunk_len:
                column = start - (keys - chunk_len) + lax.broadcasted_iota(jnp.int32, (1, chunk_keys), 1)
                s = jnp.where(column <= row, s, -jnp.inf)
            elif start > 0:
                s = s + bias_ref[0:1, start:start + chunk_keys]
            m_new = jnp.max(s, axis=-1, keepdims=True)
            if m is not None:
                m_new = jnp.maximum(m, m_new)
            p = jnp.exp2((s - m_new) * scale)
            row_sum = jnp.sum(p, axis=-1, keepdims=True)
            pv = jnp.dot(p.astype(BF16), v_ref[n, start:start + chunk_keys, :], preferred_element_type=F32)
            if m is None:
                l, acc = row_sum, pv
            else:
                fade = jnp.exp2((m - m_new) * scale)
                l, acc = l * fade + row_sum, acc * fade + pv
            m = m_new
        tile = stats_tile(rb, [m[:rb], l[:rb], m[rb:], l[rb:]])
        return acc, tile

    def stage_attend_peer(b):
        acc, tile = attend(b, other_c)
        a_send[b, :rb, 0:128] = acc[:rb]
        a_send[b, :rb, 128:256] = acc[rb:]
        rows8 = stats_rows(tile)
        a_send[b, rb:rb + STAT_ROWS, :] = jnp.concatenate([rows8, rows8], axis=1)
        copy_a(b).start()

    def stage_attend_own(b):
        acc, tile = attend(b, c)
        own_num[:, 0:128] = acc[:rb]
        own_num[:, 128:256] = acc[rb:]
        own_st[...] = tile

    def stage_core_merge(b):
        copy_a(b).wait_recv()
        peer_tile = stats_columns(a_recv[b, rb:rb + STAT_ROWS, 0:128])
        nums, columns = merge(own_num[...], own_st[...], a_recv[b, :rb, :], peer_tile, scale)
        tile = stats_tile(rb, columns)
        comb_num[:, 0:128] = nums[0]
        comb_num[:, 128:256] = nums[1]
        comb_st[...] = tile
        mine = pl.ds(pl.multiple_of(y * hb, hb), hb)
        theirs = pl.ds(pl.multiple_of(other_y * hb, hb), hb)
        y_num[b] = comb_num[mine, :]
        y_st[b] = comb_st[mine, :]
        y_send[b, :hb, :] = comb_num[theirs, :]
        rows8 = stats_rows(tile)
        y_send[b, hb:hb + STAT_ROWS, :] = jnp.concatenate([rows8, rows8], axis=1)
        copy_y(b).start()

    def stage_y_merge(b):
        copy_y(b).wait_recv()
        comb_st[...] = stats_columns(y_recv[b, hb:hb + STAT_ROWS, 0:128])
        peer_tile = comb_st[pl.ds(pl.multiple_of(y * hb, hb), hb), :]
        nums, columns = merge(y_num[b], y_st[b], y_recv[b, :hb, :], peer_tile, scale)
        o = jnp.concatenate([nums[0] / columns[1], nums[1] / columns[3]], axis=1).astype(BF16)
        o_own[b] = o
        o_send[b] = o.astype(F32)
        copy_o(b).start()

    def stage_project(b):
        copy_o(b).wait_recv()
        w_mine = w_ref[pl.ds(pl.multiple_of(c * head_cols, head_cols), head_cols), my_cols]
        w_peer = w_ref[pl.ds(pl.multiple_of(other_c * head_cols, head_cols), head_cols), my_cols]
        part = jnp.dot(o_own[b], w_mine, preferred_element_type=F32)
        p_buf[b] = part + jnp.dot(o_recv[b].astype(BF16), w_peer, preferred_element_type=F32)

        @pl.when(is_end)
        def _():
            copy_p(b).start()

    def stage_pair_sum(b):
        copy_p(b).wait_recv()
        m_send[b] = p_buf[b] + p_recv[b]
        copy_m(b).start()

    def stage_total(b):
        copy_m(b).wait_recv()
        hidden = h_ref[half_rows(b, y), my_cols].astype(F32)
        result = (hidden + (m_send[b] + m_recv[b])).astype(BF16)
        out_ref[half_rows(b, y), my_cols] = result
        f_buf[b] = result.astype(F32)
        copy_f(b).start()
        copy_yf(b).start()
        copy_d1(b).start()

    def stage_end_total(b):
        copy_f(b).wait_recv()
        copy_yf(b).start()
        copy_d1(b).start()
        out_ref[half_rows(b, y), my_cols] = f_buf[b].astype(BF16)

    def stage_y_total(b):
        copy_yf(b).wait_recv()
        copy_d2(b).start()
        out_ref[half_rows(b, other_y), my_cols] = yf_recv[b].astype(BF16)

    def stage_store(b):
        copy_d1(b).wait_recv()
        out_ref[half_rows(b, y), peer_cols] = d1_recv[b].astype(BF16)
        copy_d2(b).wait_recv()
        out_ref[half_rows(b, other_y), peer_cols] = d2_recv[b].astype(BF16)

    def stage_sent(b):
        for sent in (copy_a, copy_y, copy_o, copy_yf, copy_d1, copy_d2):
            sent(b).wait_send()

        @pl.when(is_mid)
        def _():
            copy_m(b).wait_send()
            copy_f(b).wait_send()

        @pl.when(is_end)
        def _():
            copy_p(b).wait_send()

    def run(stage, it, lag, guard=None):
        b = it - lag
        live = jnp.logical_and(b >= 0, b < nb)
        if guard is not None:
            live = jnp.logical_and(live, guard)

        @pl.when(live)
        def _():
            stage(b)

    def body(it, carry):
        run(stage_attend_peer, it, 0)
        run(stage_store, it, 10)
        run(stage_y_total, it, 9, is_end)
        run(stage_end_total, it, 7, is_end)
        run(stage_y_total, it, 7, is_mid)
        run(stage_total, it, 5, is_mid)
        run(stage_pair_sum, it, 3, is_mid)
        run(stage_y_merge, it, 1)
        run(stage_attend_own, it, 0)
        run(stage_project, it, 1)
        run(stage_core_merge, it, 0)
        return carry

    lax.fori_loop(0, nb + 11, body, 0)
    lax.fori_loop(0, nb, lambda b, carry: (stage_sent(b), carry)[1], 0)


def attend_call(q, k_all, v_all, bias, hidden, w_out, chunk_keys, scale, z_count):
    _, nb, rows2, _ = q.shape
    rb = rows2 // 2
    hb = rb // 2
    keys = k_all.shape[1]
    chunk_len, model_dim = hidden.shape
    half_cols = model_dim // 2
    heads = w_out.shape[0] // 2
    cfg = (nb, rb, keys, chunk_keys, chunk_len, scale, z_count)
    wide = pltpu.VMEM((nb, hb, half_cols), F32)
    flops = 4 * 4 * chunk_len * keys * 128 + 2 * chunk_len * w_out.shape[0] * model_dim // 4
    return pl.pallas_call(
        functools.partial(attend_kernel, cfg),
        out_shape=jax.ShapeDtypeStruct((chunk_len, model_dim), BF16),
        in_specs=[pl.BlockSpec(memory_space=pltpu.VMEM)] * 6,
        out_specs=pl.BlockSpec(memory_space=pltpu.VMEM),
        scratch_shapes=[
            pltpu.VMEM((nb, rb + STAT_ROWS, heads), F32),
            pltpu.VMEM((nb, rb + STAT_ROWS, heads), F32),
            pltpu.VMEM((rb, heads), F32),
            pltpu.VMEM((rb, 128), F32),
            pltpu.VMEM((rb, heads), F32),
            pltpu.VMEM((rb, 128), F32),
            pltpu.VMEM((nb, hb + STAT_ROWS, heads), F32),
            pltpu.VMEM((nb, hb + STAT_ROWS, heads), F32),
            pltpu.VMEM((nb, hb, heads), F32),
            pltpu.VMEM((nb, hb, 128), F32),
            pltpu.VMEM((nb, hb, heads), BF16),
            pltpu.VMEM((nb, hb, heads), F32),
            pltpu.VMEM((nb, hb, heads), F32),
            wide, wide, wide, wide, wide, wide, wide, wide,
            pltpu.SemaphoreType.DMA((9, nb)),
            pltpu.SemaphoreType.DMA((9, nb)),
        ],
        compiler_params=pltpu.CompilerParams(collective_id=0, has_side_effects=True, vmem_limit_bytes=62 * 2**20),
        cost_estimate=pl.CostEstimate(flops=flops, bytes_accessed=16 * 2**20, transcendentals=4 * chunk_len * keys),
        name="attend",
    )(q, k_all, v_all, bias, hidden, w_out)


def solution(mesh, chunk_keys=1024):
    cache_spec = P(("dp", "sp"), "tp", None)
    in_specs = (P("dp", None), P("dp"), cache_spec, cache_spec, P(None), P(None, "tp"), P(None, "tp"), P(None, "tp"), P(None), P(None), P("tp", None))
    out_specs = (P("dp", None), cache_spec, cache_spec)

    def local_step(hidden, start_pos, k_shard, v_shard, norm_gain, w_query, w_key, w_value, q_gain, k_gain, w_out):
        chunk_len, model_dim = hidden.shape
        shard_len, kv_local, head_dim = k_shard.shape
        group_size = w_query.shape[1] // head_dim // kv_local
        first_pos = start_pos[0]
        positions = first_pos + jnp.arange(chunk_len, dtype=jnp.int32)
        normed = rms_norm(hidden.astype(jnp.float32), norm_gain).astype(jnp.bfloat16)
        q_proj = jnp.dot(normed, w_query, preferred_element_type=jnp.float32).reshape(chunk_len, kv_local, group_size, head_dim)
        k_proj = jnp.dot(normed, w_key, preferred_element_type=jnp.float32).reshape(chunk_len, kv_local, head_dim)
        v_new = jnp.dot(normed, w_value, preferred_element_type=jnp.float32).reshape(chunk_len, kv_local, head_dim).astype(jnp.bfloat16)
        q_rot = rotary(rms_norm(q_proj, q_gain), positions).astype(jnp.bfloat16)
        k_rot = rotary(rms_norm(k_proj, k_gain), positions).astype(jnp.bfloat16)
        sp = lax.axis_index("sp")
        last = sp == mesh.shape["sp"] - 1
        write_at = jnp.clip(first_pos - (mesh.shape["sp"] - 1) * shard_len, 0, shard_len - chunk_len)
        old_len = shard_len - chunk_len

        def update(shard, new_rows):
            kept = lax.dynamic_slice(shard, (write_at, 0, 0), new_rows.shape)
            updated = lax.dynamic_update_slice(shard, jnp.where(last, new_rows, kept), (write_at, 0, 0))
            seen = jnp.concatenate([shard[:old_len], jnp.where(last, new_rows, shard[old_len:])], axis=0)
            return updated, jnp.transpose(seen, (1, 0, 2))

        k_upd, k_all = update(k_shard, k_rot)
        v_upd, v_all = update(v_shard, v_new)
        key_index = jnp.arange(shard_len, dtype=jnp.int32)
        bias = jnp.where(jnp.logical_or(jnp.logical_not(last), key_index < write_at), 0.0, -jnp.inf).astype(jnp.float32)[None, :]
        n_blocks = chunk_len // ROW_BLOCK
        q_blocks = q_rot.reshape(n_blocks, ROW_BLOCK, kv_local, group_size, head_dim).transpose(2, 0, 3, 1, 4)
        q_blocks = q_blocks.reshape(kv_local, n_blocks, group_size * ROW_BLOCK, head_dim)
        out = attend_call(q_blocks, k_all, v_all, bias, hidden, w_out, chunk_keys, LOG2E * head_dim ** -0.5, mesh.shape["tp"])
        return out, k_upd, v_upd

    return jax.shard_map(local_step, mesh=mesh, in_specs=in_specs, out_specs=out_specs, check_vma=False)
```

time: 548 us -> 167 us (0.30)
  waiting for transfers between devices: 307 us -> 0 us
  Pallas kernels: 0 us -> 106 us
  other arithmetic: 92.2 us -> 11.5 us
  matrix products: 63.6 us -> 8.71 us
  blocking collectives: 24.4 us -> 0 us
  between operations: 15.3 us -> 1.56 us
    psum x2 -> x0, waiting for transfers between devices: 307 us -> none  [the longest x1 266 us: local_step(): head_sum = lax.psum(head_sum, 'tp')]
    pallas_call x0 -> x1, Pallas kernels: none -> 106 us  [attend_call(): pl.pallas_call(functools.partial(attend_kernel, cfg), out_shape=jax.Shape...]
    dot_general x3 -> x0, matrix products: 50.3 us -> none  [the longest x1 27.3 us: local_step(): jnp.einsum('cngd,tnd->ncgt', q_rot, k_upd, preferred_element_type=jnp.flo...]
    concatenate x3 -> x0, other arithmetic: 35.8 us -> none  [the longest x2 35.5 us: write_rows(): extended = jnp.concatenate([zero_rows, shard, zero_rows], axis=0)]
    reduce_sum x1 -> x0, other arithmetic: 34.7 us -> none  [local_step(): denominator = jnp.sum(weights, axis=-1)]
    pmax x1 -> x0, blocking collectives: 13.7 us -> none  [local_step(): global_max = lax.pmax(jnp.max(scores, axis=-1), 'sp')]
    psum x1 -> x0, blocking collectives: 10.7 us -> none  [local_step(): denominator = lax.psum(denominator, 'sp')]
    unnamed x20 -> x29, local copies, waits for them, and re-layouts: 24.7 us -> 15.4 us
  transfers between devices with their start and end apart: 2 -> 0, of which waited for: 2 -> 0; matrix products, arithmetic and copies ran while one was open for 4% -> 0% of each run, Pallas kernels for 0% -> 0%
where the time goes in v1:
time: 167 us; the launch traced here: 166 us
  Pallas kernels  106 us (63%)
  local copies, waits for them, and re-layouts  38.5 us (23%)
  other arithmetic  11.5 us (7%)
  matrix products  8.71 us (5%)
    pallas_call x1, Pallas kernels, attend_call(): pl.pallas_call(functools.partial(attend_kernel, cfg), out_shape=jax.Shape...  106 us
    unnamed x29, local copies, waits for them, and re-layouts  15.4 us
    dynamic_update_slice x1, local copies, waits for them, and re-layouts, update(): lax.dynamic_update_slice(shard, jnp.where(last, new_rows, kept), (write_a...  7.77 us
    slice x2, local copies, waits for them, and re-layouts, update(): shard[:old_len]  5.66 us
    dot_general x1, matrix products, local_step(): jnp.dot(normed, w_value, preferred_element_type=jnp.float32)  4.51 us
    dynamic_slice x2, local copies, waits for them, and re-layouts, update(): kept = lax.dynamic_slice(shard, (write_at, 0, 0), new_rows.shape)  3.62 us

profile of v1, /device:TPU:0, one launch (start us, length us, event | category | flops | bytes accessed | tf_op | source)
XLA Modules:
  0.0 165.9 jit_solution(8500138179749590674)
XLA Ops:
  0.7 4.6 %copy.72 = bf16[4096,2,128]{2,1,0:T(2,128)(2,1)} copy(bf16[4096,2,128]{2,1,0:T(2,128)(2,1)} %param.13) | data formatting | bytes 4194304
  5.2 1.3 copy.73
  6.6 1.6 copy-done.1
  9.1 1.6 multiply_reduce_fusion.1
  10.7 1.3 copy.40
  12.0 1.6 multiply_multiply_fusion.1
  15.3 1.0 copy.41
  16.3 1.0 copy.42
  17.3 1.6 subtract_convert_fusion
  18.9 1.4 constant_dynamic-slice_fusion.1
  20.7 2.2 %constant_dynamic-slice_fusion = bf16[1024,2,128]{2,1,0:T(2,128)(2,1)} fusion(bf16[4096,2,128]{2,1,0:T(2,128)(2,1)} %copy.73, s32[]{:T(128)S(6)} %min.4), kind=kLoop, calls=%fused_computation.31 | loop fusion | bytes 1048580 | tf_op jit(solution)/shard_map/dynamic_slice | solution.py:329
  22.9 4.5 %convolution_convert_fusion = bf16[1024,256]{0,1:T(8,128)(2,1)} fusion(bf16[2048,256]{1,0:T(8,128)(2,1)S(1)} %copy-done.9, bf16[1024,2048]{1,0:T(8,128)(2,1)} %h_ref.1, f32[2048]{0:T(1024)S(1)} %copy-done.10, f32[1024]{0:T(1024)S(1)} %add_rsqrt_fusion.2), kind=kOutput, calls=%fused_computation.9 | convolution fusion | flops 1082392576 | bytes 5779456 | tf_op jit(solution)/shard_map/dot_general | solution.py:320
  27.4 1.3 copy.46
  28.8 1.1 copy_select_fusion
  29.9 2.8 %slice.26 = bf16[3072,2,128]{2,1,0:T(2,128)(2,1)S(1)} slice(bf16[4096,2,128]{2,1,0:T(2,128)(2,1)} %copy.72), slice={[0:3072], [0:2], [0:128]} | slice | bytes 3145728 | tf_op jit(solution)/shard_map/slice | solution.py:331
  32.7 2.8 %slice.30 = bf16[3072,2,128]{2,1,0:T(2,128)(2,1)S(1)} slice(bf16[4096,2,128]{2,1,0:T(2,128)(2,1)} %copy.73), slice={[0:3072], [0:2], [0:128]} | slice | bytes 3145728 | tf_op jit(solution)/shard_map/slice | solution.py:331
  35.5 7.8 %copy_dynamic-update-slice_fusion = (bf16[4096,2,128]{2,1,0:T(2,128)(2,1)}, bf16[1024,2,128]{2,1,0:T(2,128)(2,1)S(1)}, bf16[1024,2,128]{2,1,0:T(2,128)(2,1)S(1)}, bf16[4096,2,128]{2,1,0:T(2,128)(2,1)}) fusion(bf16[4096,2,128]{2,1,0:T(2,128)(2,1)} %copy.73, s32[]{:T(128)S(6)} %min.4, bf16[1024,2,128]{2,0,1:T(8,128)(2,1)S(1)} %copy_select_fusion, ...), kind=kLoop, calls=%fused_computation.22 | loop fusion | bytes 4194308 | tf_op jit(solution)/shard_map/dynamic_update_slice | solution.py:330
  43.9 1.5 maximum_bitcast_fusion.k_ref
  45.7 1.5 maximum_bitcast_fusion.1.v_ref
  47.7 1.4 copy-done.2
  49.1 2.6 %multiply_reduce_fusion = (f32[1024,2,2]{0,2,1:T(2,128)S(1)}, f32[1024,512]{0,1:T(8,128)S(1)}) fusion(bf16[2048,512]{1,0:T(8,128)(2,1)S(1)} %copy-done.8, bf16[1024,2048]{1,0:T(8,128)(2,1)S(1)} %copy-done.2, f32[2048]{0:T(1024)S(1)} %copy-done.10, f32[1024]{0:T(1024)S(1)} %add_rsqrt_fusion.2), kind=kOutput, calls=%fused_computation.8 | convolution fusion | flops 2156916736 | bytes 8417280 | tf_op jit(solution)/shard_map/dot_general | solution.py:318
  53.4 1.5 copy.38
  55.5 105.6 %attend.1 = bf16[1024,2048]{1,0:T(8,128)(2,1)} custom-call(bf16[2,8,256,128]{3,2,1,0:T(8,128)(2,1)} %bitcast.37, bf16[2,4096,128]{2,1,0:T(8,128)(2,1)} %maximum_bitcast_fusion.k_ref, bf16[2,4096,128]{2,1,0:T(8,128)(2,1)} %maximum_bitcast_fusion.1.v_ref, f32[1,4096]{1,0:T(1,128)} %or_select_fusion.bias_ref, bf16[1024,2048]{1,0:T(8,128)(2,1)} %h_ref.1, ...), custom_call_target="tpu_custom_call" | custom-call | flops 9126805504 | bytes 16777216 | tf_op jit(solution)/shard_map/attend/pallas_call | solution.py:277
  161.1 4.8 %copy.74 = bf16[1024,2048]{1,0:T(8,128)(2,1)} copy(bf16[1024,2048]{1,0:T(8,128)(2,1)} %attend.1) | data formatting | bytes 8388608
  (38 shorter events, 5.9 us)
Async XLA Ops:
  0.6 8.5 %copy-start = (bf16[2048,256]{1,0:T(8,128)(2,1)S(1)}, bf16[2048,256]{1,0:T(8,128)(2,1)}, u32[]{:S(2)}) copy-start(bf16[2048,256]{1,0:T(8,128)(2,1)} %param.17) | copy-start | bytes 3145732
  0.6 4.6 %copy-start.5 = (bf16[4096,2,128]{2,1,0:T(2,128)(2,1)S(1)}, bf16[4096,2,128]{2,1,0:T(2,128)(2,1)}, u32[]{:S(2)}) copy-start(bf16[4096,2,128]{2,1,0:T(2,128)(2,1)} %param.14) | copy-start | bytes 6291460
  5.2 2.9 %copy-start.1 = (bf16[1024,2048]{1,0:T(8,128)(2,1)S(1)}, bf16[1024,2048]{1,0:T(8,128)(2,1)}, u32[]{:S(2)}) copy-start(bf16[1024,2048]{1,0:T(8,128)(2,1)} %h_ref.1) | copy-start | bytes 12582916
  8.2 0.9 copy-start.10
  10.7 1.3 copy-start.6
  15.2 1.0 copy-start.3
  20.3 2.6 %copy-start.9 = (bf16[2048,256]{1,0:T(8,128)(2,1)S(1)}, bf16[2048,256]{1,0:T(8,128)(2,1)}, u32[]{:S(2)}) copy-start(bf16[2048,256]{1,0:T(8,128)(2,1)} %param.18) | copy-start | bytes 3145732
  45.4 2.2 %copy-start.8 = (bf16[2048,512]{1,0:T(8,128)(2,1)S(1)}, bf16[2048,512]{1,0:T(8,128)(2,1)}, u32[]{:S(2)}) copy-start(bf16[2048,512]{1,0:T(8,128)(2,1)} %param.16) | copy-start | bytes 6291460
  45.7 3.4 %copy-start.2 = (bf16[1024,2048]{1,0:T(8,128)(2,1)S(1)}, bf16[1024,2048]{1,0:T(8,128)(2,1)}, u32[]{:S(2)}) copy-start(bf16[1024,2048]{1,0:T(8,128)(2,1)} %h_ref.1) | copy-start | bytes 12582916
  49.1 2.7 %copy-start.7 = (f32[128]{0:T(128)S(1)}, f32[128]{0:T(128)}, u32[]{:S(2)}) copy-start(f32[128]{0:T(128)} %param.19) | copy-start | bytes 1540
  51.8 1.0 copy-start.4

commit v2 on v1

v2 whole, which is shorter than its diff:
```python
import functools

import jax
import jax.numpy as jnp
from jax import lax
from jax.experimental import pallas as pl
from jax.experimental.pallas import tpu as pltpu
from jax.sharding import PartitionSpec as P

ROPE_BASE = 1e6
NORM_EPS = 1e-6
LOG2E = 1.4426950408889634
MESH = pl.DeviceIdType.MESH
F32 = jnp.float32
BF16 = jnp.bfloat16
ROW_BLOCK = 128
STAT_ROWS = 8
SUBS = 4
LAG_Y = 6
LAG_PROJECT = 7
LAG_HOP = 3


def rotary_tables(positions, head_dim):
    half_dim = head_dim // 2
    inv_freq = ROPE_BASE ** (-2.0 * jnp.arange(half_dim, dtype=jnp.float32) / head_dim)
    lane = jnp.arange(head_dim)
    angles = positions.astype(jnp.float32)[:, None] * jnp.tile(inv_freq, 2)[None, :]
    return jnp.cos(angles), jnp.where(lane < half_dim, -1.0, 1.0)[None, :] * jnp.sin(angles)


def stats_tile(rows, columns):
    lane = lax.broadcasted_iota(jnp.int32, (rows, 128), 1)
    tile = jnp.zeros((rows, 128), F32)
    for k, column in enumerate(columns):
        tile = jnp.where(lane == k, column, tile)
    return tile


def stats_rows(tile):
    return jnp.transpose(tile)[:STAT_ROWS]


def stats_columns(rows8):
    return jnp.transpose(jnp.concatenate([rows8] * (128 // STAT_ROWS), axis=0))


def merge(num_a, tile_a, num_b, tile_b, scale):
    nums, columns = [], []
    for g in range(2):
        m_a, l_a = tile_a[:, 2 * g:2 * g + 1], tile_a[:, 2 * g + 1:2 * g + 2]
        m_b, l_b = tile_b[:, 2 * g:2 * g + 1], tile_b[:, 2 * g + 1:2 * g + 2]
        m = jnp.maximum(m_a, m_b)
        c_a = jnp.exp2((m_a - m) * scale)
        c_b = jnp.exp2((m_b - m) * scale)
        nums.append(num_a[:, g * 128:(g + 1) * 128] * c_a + num_b[:, g * 128:(g + 1) * 128] * c_b)
        columns += [m, l_a * c_a + l_b * c_b]
    return nums, columns


def attend_kernel(cfg, q_hbm, k_hbm, v_hbm, bias_ref, h_hbm, w_hbm, out_hbm, q_buf, k_buf, v_buf, h_buf, w_buf, out_buf, att_m, att_l, att_acc,
                  a_send, a_recv, own_num, own_st, comb_num, comb_st, y_send, y_recv, y_num, y_st, o_own, o_send, o_recv,
                  p_buf, p_recv, m_send, m_recv, f_buf, yf_recv, d1_recv, d2_recv, row_send, row_recv, sub_send, sub_recv, kv_sems, q_sems, h_sems, w_sem, out_sems):
    nb, rb, keys, chunk_keys, chunk_len, scale, z_count = cfg
    hb = rb // 2
    dp, z, sp = lax.axis_index("dp"), lax.axis_index("tp"), lax.axis_index("sp")
    y, c = lax.div(sp, 2), lax.rem(sp, 2)
    other_y, other_c = 1 - y, 1 - c
    pair_z = z + 1 - 2 * lax.rem(z, 2)
    cross_z = z_count - 1 - z
    is_mid = jnp.logical_and(z >= 1, z <= 2)
    is_end = jnp.logical_not(is_mid)
    half_cols = w_buf.shape[1]
    sub_cols = half_cols // SUBS
    head_cols = w_buf.shape[0] // 2
    core_peer = (dp, z, y * 2 + other_c)
    y_peer = (dp, z, other_y * 2 + c)
    pair_peer = (dp, pair_z, sp)
    cross_peer = (dp, cross_z, sp)
    my_cols = pl.ds(pl.multiple_of(c * half_cols, half_cols), half_cols)

    def kv_loads(n, half):
        span = pl.ds(half * (keys // 2), keys // 2)
        return (pltpu.make_async_copy(k_hbm.at[n, span], k_buf.at[n, span], kv_sems.at[0, n, half]),
                pltpu.make_async_copy(v_hbm.at[n, span], v_buf.at[n, span], kv_sems.at[1, n, half]))

    def q_load(n):
        return pltpu.make_async_copy(q_hbm.at[n], q_buf.at[n], q_sems.at[n])

    def half_rows(b, which):
        return pl.ds(pl.multiple_of(b * rb + which * hb, hb), hb)

    def h_load(b):
        return pltpu.make_async_copy(h_hbm.at[half_rows(b, y), my_cols], h_buf.at[b], h_sems.at[b])

    w_load = pltpu.make_async_copy(w_hbm.at[:, my_cols], w_buf, w_sem)

    for n in (other_c, c):
        q_load(n).start()
        for half in range(2):
            for load in kv_loads(n, half):
                load.start()
    w_load.start()

    @pl.when(is_mid)
    def _():
        for b in range(nb):
            h_load(b).start()

    barrier = pltpu.get_barrier_semaphore()
    for peer in (core_peer, y_peer, pair_peer):
        pl.semaphore_signal(barrier, inc=1, device_id=peer, device_id_type=MESH)

    @pl.when(is_mid)
    def _():
        pl.semaphore_signal(barrier, inc=1, device_id=cross_peer, device_id_type=MESH)
        pl.semaphore_wait(barrier, 4)

    @pl.when(is_end)
    def _():
        pl.semaphore_wait(barrier, 3)

    def row_copy(kind, b, src, dst, peer):
        return pltpu.make_async_remote_copy(src.at[b], dst.at[b], row_send.at[kind, b], row_recv.at[kind, b], device_id=peer, device_id_type=MESH)

    def sub_copy(kind, b, j, src, dst, peer):
        return pltpu.make_async_remote_copy(src.at[b, j], dst.at[b, j], sub_send.at[kind, b, j], sub_recv.at[kind, b, j], device_id=peer, device_id_type=MESH)

    copy_a = lambda b: row_copy(0, b, a_send, a_recv, core_peer)
    copy_y = lambda b: row_copy(1, b, y_send, y_recv, y_peer)
    copy_o = lambda b: row_copy(2, b, o_send, o_recv, core_peer)
    copy_p = lambda b, j: sub_copy(0, b, j, p_buf, p_recv, pair_peer)
    copy_m = lambda b, j: sub_copy(1, b, j, m_send, m_recv, cross_peer)
    copy_f = lambda b, j: sub_copy(2, b, j, f_buf, f_buf, pair_peer)
    copy_yf = lambda b, j: sub_copy(3, b, j, f_buf, yf_recv, y_peer)
    copy_d1 = lambda b, j: sub_copy(4, b, j, f_buf, d1_recv, core_peer)
    copy_d2 = lambda b, j: sub_copy(5, b, j, yf_recv, d2_recv, core_peer)

    def out_store(b):
        rows = pl.ds(pl.multiple_of(b * rb, rb), rb)
        return pltpu.make_async_copy(out_buf.at[rows], out_hbm.at[rows], out_sems.at[b])

    def columns_of(core, j):
        return pl.ds(pl.multiple_of(core * half_cols + j * sub_cols, sub_cols), sub_cols)

    def attend(b, n, half):
        q = q_buf[n, b]
        if half:
            m, l, acc = att_m[...], att_l[...], att_acc[...]
        else:
            m = l = acc = None
        row = b * rb + lax.rem(lax.broadcasted_iota(jnp.int32, (2 * rb, 1), 0), rb) + jnp.where(sp == 3, 0, keys)
        for start in range(half * (keys // 2), (half + 1) * (keys // 2), chunk_keys):
            s = lax.dot_general(q, k_buf[n, start:start + chunk_keys, :], (((1,), (1,)), ((), ())), preferred_element_type=F32)
            if start >= keys - chunk_len:
                column = start - (keys - chunk_len) + lax.broadcasted_iota(jnp.int32, (1, chunk_keys), 1)
                s = jnp.where(column <= row, s, -jnp.inf)
            elif start > 0:
                s = s + bias_ref[0:1, start:start + chunk_keys]
            m_new = jnp.max(s, axis=-1, keepdims=True)
            if m is not None:
                m_new = jnp.maximum(m, m_new)
            p = jnp.exp2((s - m_new) * scale)
            row_sum = jnp.sum(p, axis=-1, keepdims=True)
            pv = jnp.dot(p.astype(BF16), v_buf[n, start:start + chunk_keys, :], preferred_element_type=F32)
            if m is None:
                l, acc = row_sum, pv
            else:
                fade = jnp.exp2((m - m_new) * scale)
                l, acc = l * fade + row_sum, acc * fade + pv
            m = m_new
        if not half:
            att_m[...], att_l[...], att_acc[...] = m, l, acc
        return acc, m, l

    def stage_attend(b, piece):
        head, half = piece // 2, piece % 2
        n = c if head else other_c

        @pl.when(b == 0)
        def _():
            if half == 0:
                q_load(n).wait()
            for load in kv_loads(n, half):
                load.wait()

        acc, m, l = attend(b, n, half)
        if not half:
            return
        tile = stats_tile(rb, [m[:rb], l[:rb], m[rb:], l[rb:]])
        if head:
            own_num[:, 0:128] = acc[:rb]
            own_num[:, 128:256] = acc[rb:]
            own_st[...] = tile
        else:
            a_send[b, :rb, 0:128] = acc[:rb]
            a_send[b, :rb, 128:256] = acc[rb:]
            rows8 = stats_rows(tile)
            a_send[b, rb:rb + STAT_ROWS, :] = jnp.concatenate([rows8, rows8], axis=1)
            copy_a(b).start()

    def stage_core_merge(b):
        copy_a(b).wait_recv()
        peer_tile = stats_columns(a_recv[b, rb:rb + STAT_ROWS, 0:128])
        nums, columns = merge(own_num[...], own_st[...], a_recv[b, :rb, :], peer_tile, scale)
        tile = stats_tile(rb, columns)
        comb_num[:, 0:128] = nums[0]
        comb_num[:, 128:256] = nums[1]
        comb_st[...] = tile
        mine = pl.ds(pl.multiple_of(y * hb, hb), hb)
        theirs = pl.ds(pl.multiple_of(other_y * hb, hb), hb)
        y_send[b, :hb, :] = comb_num[theirs, :]
        rows8 = stats_rows(tile)
        y_send[b, hb:hb + STAT_ROWS, :] = jnp.concatenate([rows8, rows8], axis=1)
        copy_y(b).start()
        y_num[b] = comb_num[mine, :]
        y_st[b] = comb_st[mine, :]

    def stage_y_merge(b):
        copy_y(b).wait_recv()
        comb_st[...] = stats_columns(y_recv[b, hb:hb + STAT_ROWS, 0:128])
        peer_tile = comb_st[pl.ds(pl.multiple_of(y * hb, hb), hb), :]
        nums, columns = merge(y_num[b], y_st[b], y_recv[b, :hb, :], peer_tile, scale)
        o = jnp.concatenate([nums[0] / columns[1], nums[1] / columns[3]], axis=1).astype(BF16)
        o_send[b] = o.astype(F32)
        copy_o(b).start()
        o_own[b] = o

    def stage_project(b):
        @pl.when(b == 0)
        def _():
            w_load.wait()

        copy_o(b).wait_recv()
        w_mine = w_buf[pl.ds(pl.multiple_of(c * head_cols, head_cols), head_cols), :]
        w_peer = w_buf[pl.ds(pl.multiple_of(other_c * head_cols, head_cols), head_cols), :]
        part = jnp.dot(o_own[b], w_mine, preferred_element_type=F32)
        part = part + jnp.dot(o_recv[b].astype(BF16), w_peer, preferred_element_type=F32)
        for j in range(SUBS):
            p_buf[b, j] = part[:, j * sub_cols:(j + 1) * sub_cols]

        @pl.when(is_end)
        def _():
            for j in range(SUBS):
                copy_p(b, j).start()

    def stage_pair_sum(b, j):
        copy_p(b, j).wait_recv()
        m_send[b, j] = p_buf[b, j] + p_recv[b, j]
        copy_m(b, j).start()

    def stage_total(b, j):
        if j == 0:
            h_load(b).wait()
        copy_m(b, j).wait_recv()
        hidden = h_buf[b, :, j * sub_cols:(j + 1) * sub_cols].astype(F32)
        result = (hidden + (m_send[b, j] + m_recv[b, j])).astype(BF16)
        f_buf[b, j] = result.astype(F32)
        copy_f(b, j).start()
        copy_yf(b, j).start()
        copy_d1(b, j).start()
        out_buf[half_rows(b, y), columns_of(c, j)] = result

    def stage_end_total(b, j):
        copy_f(b, j).wait_recv()
        copy_yf(b, j).start()
        copy_d1(b, j).start()
        out_buf[half_rows(b, y), columns_of(c, j)] = f_buf[b, j].astype(BF16)

    def stage_y_total(b, j):
        copy_yf(b, j).wait_recv()
        copy_d2(b, j).start()
        out_buf[half_rows(b, other_y), columns_of(c, j)] = yf_recv[b, j].astype(BF16)

    def stage_store(b, j):
        copy_d1(b, j).wait_recv()
        out_buf[half_rows(b, y), columns_of(other_c, j)] = d1_recv[b, j].astype(BF16)
        copy_d2(b, j).wait_recv()
        out_buf[half_rows(b, other_y), columns_of(other_c, j)] = d2_recv[b, j].astype(BF16)
        if j == SUBS - 1:
            out_store(b).start()

    def stage_sent(b):
        for sent in (copy_a, copy_y, copy_o):
            sent(b).wait_send()
        out_store(b).wait()
        for j in range(SUBS):
            for sent in (copy_yf, copy_d1, copy_d2):
                sent(b, j).wait_send()

        @pl.when(is_mid)
        def _():
            for j in range(SUBS):
                copy_m(b, j).wait_send()
                copy_f(b, j).wait_send()

        @pl.when(is_end)
        def _():
            for j in range(SUBS):
                copy_p(b, j).wait_send()

    def run(stage, it, step, lag, guard=None, sub=True):
        j = (step - lag) % SUBS
        if not sub and j:
            return
        b = it + (step - lag - j) // SUBS
        live = jnp.logical_and(b >= 0, b < nb)
        if guard is not None:
            live = jnp.logical_and(live, guard)

        @pl.when(live)
        def _():
            if sub:
                stage(b, j)
            else:
                stage(b)

    lag_p, hop = LAG_PROJECT + LAG_HOP, LAG_HOP
    lag_store = lag_p + 3 * hop + 2

    def body(it, carry):
        for step in range(SUBS):
            run(stage_store, it, step, lag_store)
            run(stage_y_total, it, step, lag_p + 3 * hop, is_end)
            run(stage_end_total, it, step, lag_p + 2 * hop, is_end)
            run(stage_y_total, it, step, lag_p + 2 * hop, is_mid)
            run(stage_total, it, step, lag_p + hop, is_mid)
            run(stage_pair_sum, it, step, lag_p, is_mid)
            run(stage_attend, it, step, 0)
            run(stage_core_merge, it, step, SUBS - 1, sub=False)
            run(stage_y_merge, it, step, LAG_Y, sub=False)
            run(stage_project, it, step, LAG_PROJECT, sub=False)
        return carry

    lax.fori_loop(0, nb + (lag_store + SUBS - 1) // SUBS, body, 0)
    lax.fori_loop(0, nb, lambda b, carry: (stage_sent(b), carry)[1], 0)


def prep_kernel(cfg, pos_ref, h_hbm, gain_ref, wq_hbm, wk_hbm, wv_hbm, qg_ref, kg_ref, cos_ref, sin_ref, kc_hbm, vc_hbm,
                q_out, k_out, v_out, kc_out, vc_out, h_buf, normed, wq_buf, wkv_buf, kc_buf, vc_buf, new_buf, in_sems, cache_sems, out_sems):
    nb, rb, last_index, old_len = cfg
    chunk_len, _ = h_buf.shape
    shard_len = kc_buf.shape[0]
    kv_cols = wk_hbm.shape[1]
    is_last = lax.axis_index("sp") == last_index
    write_at = jnp.clip(pos_ref[0] - last_index * shard_len, 0, shard_len - chunk_len)
    parts = 4
    rows = chunk_len // parts

    def load(k, src, dst):
        return pltpu.make_async_copy(src, dst, in_sems.at[k])

    h_loads = [load(k, h_hbm.at[pl.ds(k * rows, rows)], h_buf.at[pl.ds(k * rows, rows)]) for k in range(parts)]
    wq_load = load(parts, wq_hbm, wq_buf)
    wk_load = load(parts + 1, wk_hbm, wkv_buf.at[:, pl.ds(0, kv_cols)])
    wv_load = load(parts + 2, wv_hbm, wkv_buf.at[:, pl.ds(kv_cols, kv_cols)])
    kc_load = pltpu.make_async_copy(kc_hbm, kc_buf, cache_sems.at[0])
    vc_load = pltpu.make_async_copy(vc_hbm, vc_buf, cache_sems.at[1])
    kc_store = pltpu.make_async_copy(kc_buf, kc_out, out_sems.at[0])
    vc_store = pltpu.make_async_copy(vc_buf, vc_out, out_sems.at[1])
    h_loads[0].start()
    kc_load.start()
    wq_load.start()
    for k in range(1, parts):
        h_loads[k].start()
    vc_load.start()

    @pl.when(is_last)
    def _():
        wk_load.start()
        wv_load.start()

    def normalize(x, gain):
        return x * lax.rsqrt(jnp.mean(x * x, axis=-1, keepdims=True) + NORM_EPS) * gain

    def rotate(x, part):
        return x * cos_ref[part * rows:(part + 1) * rows, :] + pltpu.roll(x, 64, 1) * sin_ref[part * rows:(part + 1) * rows, :]

    def split_heads(buf, out, start, stop):
        for row in range(start, stop, 256):
            x = buf[row:row + 256].reshape(256, kv_cols)
            for n in range(2):
                out[n, row:row + 256, :] = x[:, n * 128:(n + 1) * 128]

    def project_q(part):
        x = h_buf[part * rows:(part + 1) * rows, :].astype(F32)
        norm = normalize(x, gain_ref[...]).astype(BF16)
        normed[part * rows:(part + 1) * rows, :] = norm
        proj = jnp.dot(norm, wq_buf[...], preferred_element_type=F32)
        for head in range(4):
            n, g = head // 2, head % 2
            rot = rotate(normalize(proj[:, head * 128:(head + 1) * 128], qg_ref[...]), part).astype(BF16)
            for sub in range(rows // rb):
                q_out[n, part * (rows // rb) + sub, g * rb:(g + 1) * rb, :] = rot[sub * rb:(sub + 1) * rb]

    h_loads[0].wait()
    wq_load.wait()
    project_q(0)
    kc_load.wait()
    kc_store.start()
    split_heads(kc_buf, k_out, 0, old_len)
    for part in range(1, parts):
        h_loads[part].wait()
        project_q(part)
    vc_load.wait()
    vc_store.start()
    split_heads(vc_buf, v_out, 0, old_len)

    @pl.when(jnp.logical_not(is_last))
    def _():
        split_heads(kc_buf, k_out, old_len, shard_len)
        split_heads(vc_buf, v_out, old_len, shard_len)
        kc_store.wait()
        vc_store.wait()

    @pl.when(is_last)
    def _():
        wk_load.wait()
        wv_load.wait()
        for part in range(parts):
            span = slice(part * rows, (part + 1) * rows)
            proj = jnp.dot(normed[span, :], wkv_buf[...], preferred_element_type=F32)
            heads = []
            for n in range(2):
                heads.append(rotate(normalize(proj[:, n * 128:(n + 1) * 128], kg_ref[...]), part).astype(BF16))
                k_out[n, old_len + part * rows:old_len + (part + 1) * rows, :] = heads[n]
                v_out[n, old_len + part * rows:old_len + (part + 1) * rows, :] = proj[:, kv_cols + n * 128:kv_cols + (n + 1) * 128].astype(BF16)
            new_buf[0, span] = jnp.concatenate(heads, axis=1).reshape(rows, 2, 128)
            new_buf[1, span] = proj[:, kv_cols:].astype(BF16).reshape(rows, 2, 128)
        kc_store.wait()
        vc_store.wait()
        k_store = pltpu.make_async_copy(new_buf.at[0], kc_out.at[pl.ds(write_at, chunk_len)], out_sems.at[0])
        v_store = pltpu.make_async_copy(new_buf.at[1], vc_out.at[pl.ds(write_at, chunk_len)], out_sems.at[1])
        k_store.start()
        v_store.start()
        k_store.wait()
        v_store.wait()


def prep_call(start_pos, hidden, norm_gain, w_query, w_key, w_value, q_gain, k_gain, cosine, sine, k_shard, v_shard, last_index):
    chunk_len, model_dim = hidden.shape
    shard_len, kv_local, head_dim = k_shard.shape
    nb = chunk_len // ROW_BLOCK
    vmem = pl.BlockSpec(memory_space=pltpu.VMEM)
    hbm = pl.BlockSpec(memory_space=pl.ANY)
    cfg = (nb, ROW_BLOCK, last_index, shard_len - chunk_len)
    kv_shape = jax.ShapeDtypeStruct((kv_local, shard_len, head_dim), BF16)
    cache_shape = jax.ShapeDtypeStruct(k_shard.shape, BF16)
    return pl.pallas_call(
        functools.partial(prep_kernel, cfg),
        out_shape=(jax.ShapeDtypeStruct((kv_local, nb, 2 * ROW_BLOCK, head_dim), BF16), kv_shape, kv_shape, cache_shape, cache_shape),
        in_specs=[pl.BlockSpec(memory_space=pltpu.SMEM), hbm, vmem, hbm, hbm, hbm, vmem, vmem, vmem, vmem, hbm, hbm],
        out_specs=(vmem, vmem, vmem, hbm, hbm),
        scratch_shapes=[
            pltpu.VMEM((chunk_len, model_dim), BF16),
            pltpu.VMEM((chunk_len, model_dim), BF16),
            pltpu.VMEM(w_query.shape, BF16),
            pltpu.VMEM((model_dim, 2 * w_key.shape[1]), BF16),
            pltpu.VMEM(k_shard.shape, BF16),
            pltpu.VMEM(k_shard.shape, BF16),
            pltpu.VMEM((2, chunk_len, kv_local, head_dim), BF16),
            pltpu.SemaphoreType.DMA((7,)),
            pltpu.SemaphoreType.DMA((2,)),
            pltpu.SemaphoreType.DMA((2,)),
        ],
        compiler_params=pltpu.CompilerParams(vmem_limit_bytes=48 * 2**20),
        cost_estimate=pl.CostEstimate(flops=2 * chunk_len * model_dim * 1024, bytes_accessed=24 * 2**20, transcendentals=0),
        name="prep",
    )(start_pos, hidden, norm_gain[None, :], w_query, w_key, w_value, q_gain[None, :], k_gain[None, :], cosine, sine, k_shard, v_shard)


def attend_call(q, k_all, v_all, bias, hidden, w_out, chunk_keys, scale, z_count):
    _, nb, rows2, _ = q.shape
    rb = rows2 // 2
    hb = rb // 2
    keys = k_all.shape[1]
    chunk_len, model_dim = hidden.shape
    half_cols = model_dim // 2
    heads = w_out.shape[0] // 2
    cfg = (nb, rb, keys, chunk_keys, chunk_len, scale, z_count)
    sub = pltpu.VMEM((nb, SUBS, hb, half_cols // SUBS), F32)
    flops = 4 * 4 * chunk_len * keys * 128 + 2 * chunk_len * w_out.shape[0] * model_dim // 4
    vmem = pl.BlockSpec(memory_space=pltpu.VMEM)
    hbm = pl.BlockSpec(memory_space=pl.ANY)
    return pl.pallas_call(
        functools.partial(attend_kernel, cfg),
        out_shape=jax.ShapeDtypeStruct((chunk_len, model_dim), BF16),
        in_specs=[hbm, hbm, hbm, vmem, hbm, hbm],
        out_specs=hbm,
        scratch_shapes=[
            pltpu.VMEM(q.shape, BF16),
            pltpu.VMEM(k_all.shape, BF16),
            pltpu.VMEM(v_all.shape, BF16),
            pltpu.VMEM((nb, hb, half_cols), BF16),
            pltpu.VMEM((w_out.shape[0], half_cols), BF16),
            pltpu.VMEM((chunk_len, model_dim), BF16),
            pltpu.VMEM((2 * rb, 1), F32),
            pltpu.VMEM((2 * rb, 1), F32),
            pltpu.VMEM((2 * rb, 128), F32),
            pltpu.VMEM((nb, rb + STAT_ROWS, heads), F32),
            pltpu.VMEM((nb, rb + STAT_ROWS, heads), F32),
            pltpu.VMEM((rb, heads), F32),
            pltpu.VMEM((rb, 128), F32),
            pltpu.VMEM((rb, heads), F32),
            pltpu.VMEM((rb, 128), F32),
            pltpu.VMEM((nb, hb + STAT_ROWS, heads), F32),
            pltpu.VMEM((nb, hb + STAT_ROWS, heads), F32),
            pltpu.VMEM((nb, hb, heads), F32),
            pltpu.VMEM((nb, hb, 128), F32),
            pltpu.VMEM((nb, hb, heads), BF16),
            pltpu.VMEM((nb, hb, heads), F32),
            pltpu.VMEM((nb, hb, heads), F32),
            sub, sub, sub, sub, sub, sub, sub, sub,
            pltpu.SemaphoreType.DMA((3, nb)),
            pltpu.SemaphoreType.DMA((3, nb)),
            pltpu.SemaphoreType.DMA((6, nb, SUBS)),
            pltpu.SemaphoreType.DMA((6, nb, SUBS)),
            pltpu.SemaphoreType.DMA((2, 2, 2)),
            pltpu.SemaphoreType.DMA((2,)),
            pltpu.SemaphoreType.DMA((nb,)),
            pltpu.SemaphoreType.DMA,
            pltpu.SemaphoreType.DMA((nb,)),
        ],
        compiler_params=pltpu.CompilerParams(collective_id=0, has_side_effects=True, vmem_limit_bytes=56 * 2**20),
        cost_estimate=pl.CostEstimate(flops=flops, bytes_accessed=16 * 2**20, transcendentals=4 * chunk_len * keys),
        name="attend",
    )(q, k_all, v_all, bias, hidden, w_out)


def solution(mesh, chunk_keys=1024):
    cache_spec = P(("dp", "sp"), "tp", None)
    in_specs = (P("dp", None), P("dp"), cache_spec, cache_spec, P(None), P(None, "tp"), P(None, "tp"), P(None, "tp"), P(None), P(None), P("tp", None))
    out_specs = (P("dp", None), cache_spec, cache_spec)

    def local_step(hidden, start_pos, k_shard, v_shard, norm_gain, w_query, w_key, w_value, q_gain, k_gain, w_out):
        chunk_len, model_dim = hidden.shape
        shard_len, kv_local, head_dim = k_shard.shape
        last_index = mesh.shape["sp"] - 1
        positions = start_pos[0] + jnp.arange(chunk_len, dtype=jnp.int32)
        cosine, sine = rotary_tables(positions, head_dim)
        q_blocks, k_all, v_all, k_upd, v_upd = prep_call(start_pos, hidden, norm_gain, w_query, w_key, w_value, q_gain, k_gain, cosine, sine, k_shard, v_shard, last_index)
        key_index = jnp.arange(shard_len, dtype=jnp.int32)
        seen = jnp.logical_or(lax.axis_index("sp") != last_index, key_index < start_pos[0] - last_index * shard_len)
        bias = jnp.where(seen, 0.0, -jnp.inf).astype(jnp.float32)[None, :]
        out = attend_call(q_blocks, k_all, v_all, bias, hidden, w_out, chunk_keys, LOG2E * head_dim ** -0.5, mesh.shape["tp"])
        return out, k_upd, v_upd

    return jax.shard_map(local_step, mesh=mesh, in_specs=in_specs, out_specs=out_specs, check_vma=False)
```

time: 167 us -> 120 us (0.72)
  local copies, waits for them, and re-layouts: 38.5 us -> 10.3 us
  other arithmetic: 11.5 us -> 2.54 us
  matrix products: 8.71 us -> 0 us
    pallas_call x1, Pallas kernels: 106 us -> 91.7 us  [attend_call(): pl.pallas_call(functools.partial(attend_kernel, cfg), out_shape=jax.Shape...]
    pallas_call x0 -> x1, Pallas kernels: none -> 13.4 us  [prep_call(): pl.pallas_call(functools.partial(prep_kernel, cfg), out_shape=(jax.ShapeD...]
    dot_general x3 -> x0, matrix products: 8.71 us -> none  [the longest x1 4.51 us: local_step(): jnp.dot(normed, w_value, preferred_element_type=jnp.float32)]
    dynamic_update_slice x1 -> x0, local copies, waits for them, and re-layouts: 7.77 us -> none  [update(): lax.dynamic_update_slice(shard, jnp.where(last, new_rows, kept), (write_a...]
    slice x2 -> x0, local copies, waits for them, and re-layouts: 5.66 us -> none  [update(): shard[:old_len]]
    unnamed x29 -> x13, local copies, waits for them, and re-layouts: 15.4 us -> 10.2 us
    dynamic_slice x2 -> x0, local copies, waits for them, and re-layouts: 3.62 us -> none  [update(): kept = lax.dynamic_slice(shard, (write_at, 0, 0), new_rows.shape)]
    transpose x3 -> x0, other arithmetic: 3.01 us -> none  [the longest x2 2.92 us: update(): return (updated, jnp.transpose(seen, (1, 0, 2)))]
where the time goes in v2:
time: 120 us; the launch traced here: 119 us
  Pallas kernels  105 us (88%)
  local copies, waits for them, and re-layouts  10.3 us (9%)
  other arithmetic  2.54 us (2%)
  between operations  1.34 us (1%)
    pallas_call x1, Pallas kernels, attend_call(): pl.pallas_call(functools.partial(attend_kernel, cfg), out_shape=jax.Shape...  91.7 us
    pallas_call x1, Pallas kernels, prep_call(): pl.pallas_call(functools.partial(prep_kernel, cfg), out_shape=(jax.ShapeD...  13.4 us
    unnamed x13, local copies, waits for them, and re-layouts  10.2 us

profile of v2, /device:TPU:0, one launch (start us, length us, event | category | flops | bytes accessed | tf_op | source)
XLA Modules:
  0.0 119.3 jit_solution(17356689322371557314)
XLA Ops:
  1.3 0.1 mul.27
  1.4 0.6 or_select_fusion.bias_ref
  2.0 1.9 %fusion = (f32[1024,128]{1,0:T(8,128)S(1)}, f32[1024,128]{1,0:T(8,128)S(1)}) fusion(f32[128]{0:T(128)S(1)} %compare_select_fusion, f32[128]{0:T(128)S(1)} %mul.27, f32[1024]{0:T(1024)S(1)} %add_convert_fusion), kind=kLoop, calls=%fused_computation.2 | loop fusion | flops 262144 | bytes 1053696 | tf_op jit(solution)/shard_map/mul | solution.py:29
  3.9 0.0 copy-start
  3.9 1.2 %copy-done = bf16[2048,256]{1,0:T(8,128)(2,1)S(1)} copy-done((bf16[2048,256]{1,0:T(8,128)(2,1)S(1)}, bf16[2048,256]{1,0:T(8,128)(2,1)}, u32[]{:S(2)}) %copy-start) | copy-done | bytes 1048600
  5.2 0.0 copy-start.1
  5.2 1.2 %copy-done.1 = bf16[2048,256]{1,0:T(8,128)(2,1)S(1)} copy-done((bf16[2048,256]{1,0:T(8,128)(2,1)S(1)}, bf16[2048,256]{1,0:T(8,128)(2,1)}, u32[]{:S(2)}) %copy-start.1) | copy-done | bytes 1048600
  6.4 0.0 copy-start.2
  6.4 0.7 copy-done.2
  7.1 0.0 copy-start.3
  7.1 0.7 copy-done.3
  7.7 0.0 copy-start.4
  7.7 0.7 copy-done.4
  8.4 13.4 %prep.1 = (bf16[2,8,256,128]{3,2,1,0:T(8,128)(2,1)S(1)}, bf16[2,4096,128]{2,1,0:T(8,128)(2,1)}, bf16[2,4096,128]{2,1,0:T(8,128)(2,1)}, bf16[4096,2,128]{2,1,0:T(2,128)(2,1)}, bf16[4096,2,128]{2,1,0:T(2,128)(2,1)}) custom-call(s32[1]{0:T(128)} %copy.15.pos_ref, bf16[1024,2048]{1,0:T(8,128)(2,1)} %h_hbm.3, f32[1,2048]{1,0:T(1,128)S(1)} %bitcast.6, ...), custom_call_target="tpu_custom_call" | custom-call | flops 4294967296 | bytes 25165824 | tf_op jit(solution)/shard_map/prep/pallas_call | solution.py:449
  21.8 0.0 copy-start.5
  21.8 1.0 copy-done.5
  22.8 91.7 %attend.1 = bf16[1024,2048]{1,0:T(8,128)(2,1)} custom-call(bf16[2,8,256,128]{3,2,1,0:T(8,128)(2,1)} %copy-done.5, bf16[2,4096,128]{2,1,0:T(8,128)(2,1)} %get-tuple-element.9.k_hbm, bf16[2,4096,128]{2,1,0:T(8,128)(2,1)} %get-tuple-element.10.v_hbm, f32[1,4096]{1,0:T(1,128)} %or_select_fusion.bias_ref, bf16[1024,2048]{1,0:T(8,128)(2,1)} %h_hbm.3, ...), custom_call_target="tpu_custom_call" | custom-call | flops 9126805504 | bytes 16777216 | tf_op jit(solution)/shard_map/attend/pallas_call | solution.py:485
  114.5 4.8 %copy.16 = bf16[1024,2048]{1,0:T(8,128)(2,1)} copy(bf16[1024,2048]{1,0:T(8,128)(2,1)} %attend.1) | data formatting | bytes 8388608
  (4 shorter events, 0.0 us)
Async XLA Ops:
  3.9 1.2 %copy-start = (bf16[2048,256]{1,0:T(8,128)(2,1)S(1)}, bf16[2048,256]{1,0:T(8,128)(2,1)}, u32[]{:S(2)}) copy-start(bf16[2048,256]{1,0:T(8,128)(2,1)} %wk_hbm.1) | copy-start | bytes 3145732
  5.2 1.2 %copy-start.1 = (bf16[2048,256]{1,0:T(8,128)(2,1)S(1)}, bf16[2048,256]{1,0:T(8,128)(2,1)}, u32[]{:S(2)}) copy-start(bf16[2048,256]{1,0:T(8,128)(2,1)} %wv_hbm.1) | copy-start | bytes 3145732
  6.4 0.7 copy-start.2
  7.1 0.7 copy-start.3
  7.7 0.7 copy-start.4
  21.8 1.0 copy-start.5

commit v3 on v2

v3 whole, which is shorter than its diff:
```python
import functools

import jax
import jax.numpy as jnp
from jax import lax
from jax.experimental import pallas as pl
from jax.experimental.pallas import tpu as pltpu
from jax.sharding import PartitionSpec as P

ROPE_BASE = 1e6
NORM_EPS = 1e-6
LOG2E = 1.4426950408889634
MESH = pl.DeviceIdType.MESH
F32 = jnp.float32
BF16 = jnp.bfloat16
ROW_BLOCK = 128
STAT_ROWS = 8
SUBS = 4
LAG_Y = 6
LAG_PROJECT = 7
LAG_HOP = 3
LAST_SHARD = 3


def rotary_tables(positions, head_dim):
    half_dim = head_dim // 2
    inv_freq = ROPE_BASE ** (-2.0 * jnp.arange(half_dim, dtype=jnp.float32) / head_dim)
    lane = jnp.arange(head_dim)
    angles = positions.astype(jnp.float32)[:, None] * jnp.tile(inv_freq, 2)[None, :]
    return jnp.cos(angles), jnp.where(lane < half_dim, -1.0, 1.0)[None, :] * jnp.sin(angles)


def stats_tile(rows, columns):
    lane = lax.broadcasted_iota(jnp.int32, (rows, 128), 1)
    tile = jnp.zeros((rows, 128), F32)
    for k, column in enumerate(columns):
        tile = jnp.where(lane == k, column, tile)
    return tile


def stats_rows(tile):
    return jnp.transpose(tile)[:STAT_ROWS]


def stats_columns(rows8):
    return jnp.transpose(jnp.concatenate([rows8] * (128 // STAT_ROWS), axis=0))


def merge(num_a, tile_a, num_b, tile_b, scale):
    nums, columns = [], []
    for g in range(2):
        m_a, l_a = tile_a[:, 2 * g:2 * g + 1], tile_a[:, 2 * g + 1:2 * g + 2]
        m_b, l_b = tile_b[:, 2 * g:2 * g + 1], tile_b[:, 2 * g + 1:2 * g + 2]
        m = jnp.maximum(m_a, m_b)
        c_a = jnp.exp2((m_a - m) * scale)
        c_b = jnp.exp2((m_b - m) * scale)
        nums.append(num_a[:, g * 128:(g + 1) * 128] * c_a + num_b[:, g * 128:(g + 1) * 128] * c_b)
        columns += [m, l_a * c_a + l_b * c_b]
    return nums, columns


def attend_kernel(cfg, pos_ref, h_hbm, gain_ref, wq_hbm, wk_hbm, wv_hbm, qg_ref, kg_ref, cos_ref, sin_ref, kc_hbm, vc_hbm, w_hbm, out_hbm, kn_hbm, vn_hbm,
                  h_buf, wq_buf, wkv_buf, kc_buf, vc_buf, k_buf, v_buf, new_buf, q_buf, bias_ref, w_buf, out_buf, att_m, att_l, att_acc,
                  a_send, a_recv, own_num, own_st, comb_num, comb_st, y_send, y_recv, y_num, y_st, o_own, o_send, o_recv,
                  p_buf, p_recv, m_send, m_recv, f_buf, yf_recv, d1_recv, d2_recv, row_send, row_recv, sub_send, sub_recv,
                  kv_sems, w_sems, h_sems, new_sems, out_sems):
    nb, rb, keys, chunk_keys, chunk_len, scale, z_count = cfg
    hb = rb // 2
    dp, z, sp = lax.axis_index("dp"), lax.axis_index("tp"), lax.axis_index("sp")
    y, c = lax.div(sp, 2), lax.rem(sp, 2)
    other_y, other_c = 1 - y, 1 - c
    pair_z = z + 1 - 2 * lax.rem(z, 2)
    cross_z = z_count - 1 - z
    is_mid = jnp.logical_and(z >= 1, z <= 2)
    is_end = jnp.logical_not(is_mid)
    half_cols = w_buf.shape[1]
    sub_cols = half_cols // SUBS
    head_cols = w_buf.shape[0] // 2
    core_peer = (dp, z, y * 2 + other_c)
    y_peer = (dp, z, other_y * 2 + c)
    pair_peer = (dp, pair_z, sp)
    cross_peer = (dp, cross_z, sp)
    my_cols = pl.ds(pl.multiple_of(c * half_cols, half_cols), half_cols)

    last = sp == LAST_SHARD
    old_len = keys - chunk_len
    kv_cols = wk_hbm.shape[1]
    limit = jnp.where(last, pos_ref[0] - LAST_SHARD * keys, keys)

    def half_rows(b, which):
        return pl.ds(pl.multiple_of(b * rb + which * hb, hb), hb)

    def block_rows(b, rows):
        return pl.ds(pl.multiple_of(b * rows, rows), rows)

    def cache_loads(half):
        span = pl.ds(half * (keys // 2), keys // 2)
        return (pltpu.make_async_copy(kc_hbm.at[span], kc_buf.at[span], kv_sems.at[0, half]),
                pltpu.make_async_copy(vc_hbm.at[span], vc_buf.at[span], kv_sems.at[1, half]))

    def h_load(b):
        return pltpu.make_async_copy(h_hbm.at[block_rows(b, rb)], h_buf.at[block_rows(b, rb)], h_sems.at[b])

    wq_load = pltpu.make_async_copy(wq_hbm, wq_buf, w_sems.at[0])
    wk_load = pltpu.make_async_copy(wk_hbm, wkv_buf.at[:, pl.ds(0, kv_cols)], w_sems.at[1])
    wv_load = pltpu.make_async_copy(wv_hbm, wkv_buf.at[:, pl.ds(kv_cols, kv_cols)], w_sems.at[2])
    w_load = pltpu.make_async_copy(w_hbm.at[:, my_cols], w_buf, w_sems.at[3])
    kn_store = pltpu.make_async_copy(new_buf.at[0], kn_hbm, new_sems.at[0])
    vn_store = pltpu.make_async_copy(new_buf.at[1], vn_hbm, new_sems.at[1])

    @pl.when(last)
    def _():
        wk_load.start()
        wv_load.start()

    h_load(0).start()
    h_load(1).start()
    wq_load.start()
    for half in range(2):
        for load in cache_loads(half):
            load.start()
    for b in range(2, nb):
        h_load(b).start()
    w_load.start()

    barrier = pltpu.get_barrier_semaphore()
    for peer in (core_peer, y_peer, pair_peer):
        pl.semaphore_signal(barrier, inc=1, device_id=peer, device_id_type=MESH)

    @pl.when(is_mid)
    def _():
        pl.semaphore_signal(barrier, inc=1, device_id=cross_peer, device_id_type=MESH)
        pl.semaphore_wait(barrier, 4)

    @pl.when(is_end)
    def _():
        pl.semaphore_wait(barrier, 3)

    key_index = lax.broadcasted_iota(jnp.int32, (1, keys), 1)
    bias_ref[...] = jnp.where(key_index < limit, 0.0, -jnp.inf).astype(F32)

    def normalize(x, gain):
        return x * lax.rsqrt(jnp.mean(x * x, axis=-1, keepdims=True) + NORM_EPS) * gain

    def rotate(x, span):
        return (x * cos_ref[span, :] + pltpu.roll(x, 64, 1) * sin_ref[span, :]).astype(BF16)

    def project_q(b):
        @pl.when(jnp.logical_not(last))
        def _():
            h_load(b).wait()

        @pl.when(b == 0)
        def _():
            wq_load.wait()

        span = block_rows(b, rb)
        normed = normalize(h_buf[span, :].astype(F32), gain_ref[...]).astype(BF16)
        proj = jnp.dot(normed, wq_buf[...], preferred_element_type=F32)
        for head in range(4):
            q_buf[head // 2, (head % 2) * rb:(head % 2 + 1) * rb, :] = rotate(normalize(proj[:, head * 128:(head + 1) * 128], qg_ref[...]), span)

    def project_new(part, carry):
        rows = 2 * rb
        for b in range(2):
            h_load(2 * part + b).wait()
        span = block_rows(part, rows)
        normed = normalize(h_buf[span, :].astype(F32), gain_ref[...]).astype(BF16)
        proj = jnp.dot(normed, wkv_buf[...], preferred_element_type=F32)
        place = pl.ds(pl.multiple_of(old_len + part * rows, rows), rows)
        heads = []
        for n in range(2):
            heads.append(rotate(normalize(proj[:, n * 128:(n + 1) * 128], kg_ref[...]), span))
            k_buf[n, place, :] = heads[n]
            v_buf[n, place, :] = proj[:, kv_cols + n * 128:kv_cols + (n + 1) * 128].astype(BF16)
        new_buf[0, span] = jnp.concatenate(heads, axis=1).reshape(rows, 2, 128)
        new_buf[1, span] = proj[:, kv_cols:].astype(BF16).reshape(rows, 2, 128)
        return carry

    def split_heads(start, stop):
        for src, dst in ((kc_buf, k_buf), (vc_buf, v_buf)):
            for row in range(start, stop, 256):
                x = src[row:row + 256].reshape(256, kv_cols)
                for n in range(2):
                    dst[n, row:row + 256, :] = x[:, n * 128:(n + 1) * 128]

    def prepare_keys(half):
        for load in cache_loads(half):
            load.wait()
        if half == 0:
            split_heads(0, keys // 2)
        else:
            split_heads(keys // 2, old_len)

            @pl.when(jnp.logical_not(last))
            def _():
                split_heads(old_len, keys)

    @pl.when(last)
    def _():
        wk_load.wait()
        wv_load.wait()
        lax.fori_loop(0, chunk_len // (2 * rb), project_new, 0)
        kn_store.start()
        vn_store.start()

    def row_copy(kind, b, src, dst, peer):
        return pltpu.make_async_remote_copy(src.at[b], dst.at[b], row_send.at[kind, b], row_recv.at[kind, b], device_id=peer, device_id_type=MESH)

    def sub_copy(kind, b, j, src, dst, peer):
        return pltpu.make_async_remote_copy(src.at[b, j], dst.at[b, j], sub_send.at[kind, b, j], sub_recv.at[kind, b, j], device_id=peer, device_id_type=MESH)

    copy_a = lambda b: row_copy(0, b, a_send, a_recv, core_peer)
    copy_y = lambda b: row_copy(1, b, y_send, y_recv, y_peer)
    copy_o = lambda b: row_copy(2, b, o_send, o_recv, core_peer)
    copy_p = lambda b, j: sub_copy(0, b, j, p_buf, p_recv, pair_peer)
    copy_m = lambda b, j: sub_copy(1, b, j, m_send, m_recv, cross_peer)
    copy_f = lambda b, j: sub_copy(2, b, j, f_buf, f_buf, pair_peer)
    copy_yf = lambda b, j: sub_copy(3, b, j, f_buf, yf_recv, y_peer)
    copy_d1 = lambda b, j: sub_copy(4, b, j, f_buf, d1_recv, core_peer)
    copy_d2 = lambda b, j: sub_copy(5, b, j, yf_recv, d2_recv, core_peer)

    def out_store(b):
        rows = pl.ds(pl.multiple_of(b * rb, rb), rb)
        return pltpu.make_async_copy(out_buf.at[rows], out_hbm.at[rows], out_sems.at[b])

    def columns_of(core, j):
        return pl.ds(pl.multiple_of(core * half_cols + j * sub_cols, sub_cols), sub_cols)

    def attend(b, n, half):
        q = q_buf[n]
        row = b * rb + lax.rem(lax.broadcasted_iota(jnp.int32, (2 * rb, 1), 0), rb) + jnp.where(last, 0, keys)
        first, width = half * (keys // 2), keys // 2
        scores = lax.dot_general(q, k_buf[n, first:first + width, :], (((1,), (1,)), ((), ())), preferred_element_type=F32)
        parts = []
        for start in range(0, width, chunk_keys):
            s, key = scores[:, start:start + chunk_keys], first + start
            if key >= keys - chunk_len:
                column = key - (keys - chunk_len) + lax.broadcasted_iota(jnp.int32, (1, chunk_keys), 1)
                s = jnp.where(column <= row, s, -jnp.inf)
            elif key > 0:
                s = s + bias_ref[0:1, key:key + chunk_keys]
            parts.append(s)
        m = jnp.max(functools.reduce(jnp.maximum, parts), axis=-1, keepdims=True)
        if half:
            m = jnp.maximum(m, att_m[...])
        weights = [jnp.exp2((s - m) * scale) for s in parts]
        l = jnp.sum(functools.reduce(jnp.add, weights), axis=-1, keepdims=True)
        acc = jnp.dot(jnp.concatenate([p.astype(BF16) for p in weights], axis=1), v_buf[n, first:first + width, :], preferred_element_type=F32)
        if half:
            fade = jnp.exp2((att_m[...] - m) * scale)
            l, acc = att_l[...] * fade + l, att_acc[...] * fade + acc
        if not half:
            att_m[...], att_l[...], att_acc[...] = m, l, acc
        return acc, m, l

    def stage_attend(b, piece):
        head, half = piece // 2, piece % 2
        n = c if head else other_c

        if piece == 0:
            project_q(b)
        if head == 0:
            @pl.when(b == 0)
            def _():
                prepare_keys(half)

        acc, m, l = attend(b, n, half)
        if not half:
            return
        tile = stats_tile(rb, [m[:rb], l[:rb], m[rb:], l[rb:]])
        if head:
            own_num[:, 0:128] = acc[:rb]
            own_num[:, 128:256] = acc[rb:]
            own_st[...] = tile
        else:
            a_send[b, :rb, 0:128] = acc[:rb]
            a_send[b, :rb, 128:256] = acc[rb:]
            rows8 = stats_rows(tile)
            a_send[b, rb:rb + STAT_ROWS, :] = jnp.concatenate([rows8, rows8], axis=1)
            copy_a(b).start()

    def stage_core_merge(b):
        copy_a(b).wait_recv()
        peer_tile = stats_columns(a_recv[b, rb:rb + STAT_ROWS, 0:128])
        nums, columns = merge(own_num[...], own_st[...], a_recv[b, :rb, :], peer_tile, scale)
        tile = stats_tile(rb, columns)
        comb_num[:, 0:128] = nums[0]
        comb_num[:, 128:256] = nums[1]
        comb_st[...] = tile
        mine = pl.ds(pl.multiple_of(y * hb, hb), hb)
        theirs = pl.ds(pl.multiple_of(other_y * hb, hb), hb)
        y_send[b, :hb, :] = comb_num[theirs, :]
        rows8 = stats_rows(tile)
        y_send[b, hb:hb + STAT_ROWS, :] = jnp.concatenate([rows8, rows8], axis=1)
        copy_y(b).start()
        y_num[b] = comb_num[mine, :]
        y_st[b] = comb_st[mine, :]

    def stage_y_merge(b):
        copy_y(b).wait_recv()
        comb_st[...] = stats_columns(y_recv[b, hb:hb + STAT_ROWS, 0:128])
        peer_tile = comb_st[pl.ds(pl.multiple_of(y * hb, hb), hb), :]
        nums, columns = merge(y_num[b], y_st[b], y_recv[b, :hb, :], peer_tile, scale)
        o = jnp.concatenate([nums[0] / columns[1], nums[1] / columns[3]], axis=1).astype(BF16)
        o_send[b] = o.astype(F32)
        copy_o(b).start()
        o_own[b] = o

    def stage_project(b):
        @pl.when(b == 0)
        def _():
            w_load.wait()

        copy_o(b).wait_recv()
        w_mine = w_buf[pl.ds(pl.multiple_of(c * head_cols, head_cols), head_cols), :]
        w_peer = w_buf[pl.ds(pl.multiple_of(other_c * head_cols, head_cols), head_cols), :]
        part = jnp.dot(o_own[b], w_mine, preferred_element_type=F32)
        part = part + jnp.dot(o_recv[b].astype(BF16), w_peer, preferred_element_type=F32)
        for j in range(SUBS):
            p_buf[b, j] = part[:, j * sub_cols:(j + 1) * sub_cols]

        @pl.when(is_end)
        def _():
            for j in range(SUBS):
                copy_p(b, j).start()

    def stage_pair_sum(b, j):
        copy_p(b, j).wait_recv()
        m_send[b, j] = p_buf[b, j] + p_recv[b, j]
        copy_m(b, j).start()

    def stage_total(b, j):
        copy_m(b, j).wait_recv()
        hidden = h_buf[half_rows(b, y), columns_of(c, j)].astype(F32)
        result = (hidden + (m_send[b, j] + m_recv[b, j])).astype(BF16)
        f_buf[b, j] = result.astype(F32)
        copy_f(b, j).start()
        copy_yf(b, j).start()
        copy_d1(b, j).start()
        out_buf[half_rows(b, y), columns_of(c, j)] = result

    def stage_end_total(b, j):
        copy_f(b, j).wait_recv()
        copy_yf(b, j).start()
        copy_d1(b, j).start()
        out_buf[half_rows(b, y), columns_of(c, j)] = f_buf[b, j].astype(BF16)

    def stage_y_total(b, j):
        copy_yf(b, j).wait_recv()
        copy_d2(b, j).start()
        out_buf[half_rows(b, other_y), columns_of(c, j)] = yf_recv[b, j].astype(BF16)

    def stage_store(b, j):
        copy_d1(b, j).wait_recv()
        out_buf[half_rows(b, y), columns_of(other_c, j)] = d1_recv[b, j].astype(BF16)
        copy_d2(b, j).wait_recv()
        out_buf[half_rows(b, other_y), columns_of(other_c, j)] = d2_recv[b, j].astype(BF16)
        if j == SUBS - 1:
            out_store(b).start()

    def stage_sent(b):
        for sent in (copy_a, copy_y, copy_o):
            sent(b).wait_send()
        out_store(b).wait()
        for j in range(SUBS):
            for sent in (copy_yf, copy_d1, copy_d2):
                sent(b, j).wait_send()

        @pl.when(is_mid)
        def _():
            for j in range(SUBS):
                copy_m(b, j).wait_send()
                copy_f(b, j).wait_send()

        @pl.when(is_end)
        def _():
            for j in range(SUBS):
                copy_p(b, j).wait_send()

    def run(stage, it, step, lag, guard=None, sub=True):
        j = (step - lag) % SUBS
        if not sub and j:
            return
        b = it + (step - lag - j) // SUBS
        live = jnp.logical_and(b >= 0, b < nb)
        if guard is not None:
            live = jnp.logical_and(live, guard)

        @pl.when(live)
        def _():
            if sub:
                stage(b, j)
            else:
                stage(b)

    lag_p, hop = LAG_PROJECT + LAG_HOP, LAG_HOP
    lag_store = lag_p + 3 * hop + 2

    def body(it, carry):
        for step in range(SUBS):
            run(stage_store, it, step, lag_store)
            run(stage_y_total, it, step, lag_p + 3 * hop, is_end)
            run(stage_end_total, it, step, lag_p + 2 * hop, is_end)
            run(stage_y_total, it, step, lag_p + 2 * hop, is_mid)
            run(stage_total, it, step, lag_p + hop, is_mid)
            run(stage_pair_sum, it, step, lag_p, is_mid)
            run(stage_attend, it, step, 0)
            run(stage_core_merge, it, step, SUBS - 1, sub=False)
            run(stage_y_merge, it, step, LAG_Y, sub=False)
            run(stage_project, it, step, LAG_PROJECT, sub=False)
        return carry

    lax.fori_loop(0, nb + (lag_store + SUBS - 1) // SUBS, body, 0)
    lax.fori_loop(0, nb, lambda b, carry: (stage_sent(b), carry)[1], 0)

    @pl.when(last)
    def _():
        kn_store.wait()
        vn_store.wait()


def finish_kernel(cfg, pos_ref, kc_hbm, vc_hbm, kn_hbm, vn_hbm, x_hbm, kc_out, vc_out, x_out, kc_buf, vc_buf, kn_buf, vn_buf, x_buf, in_sems, out_sems):
    last_index, parts = cfg
    is_last = lax.axis_index("sp") == last_index
    shard_len, chunk_len = kc_buf.shape[0], kn_buf.shape[0]
    write_at = jnp.clip(pos_ref[0] - last_index * shard_len, 0, shard_len - chunk_len)
    jobs = []
    for src, buf, dst in ((kc_hbm, kc_buf, kc_out), (vc_hbm, vc_buf, vc_out), (x_hbm, x_buf, x_out)):
        rows = buf.shape[0] // parts
        for part in range(parts):
            span = pl.ds(part * rows, rows)
            k = len(jobs)
            jobs.append((pltpu.make_async_copy(src.at[span], buf.at[span], in_sems.at[k]), pltpu.make_async_copy(buf.at[span], dst.at[span], out_sems.at[k])))
    k = len(jobs)
    new_loads = [pltpu.make_async_copy(kn_hbm, kn_buf, in_sems.at[k]), pltpu.make_async_copy(vn_hbm, vn_buf, in_sems.at[k + 1])]
    new_stores = [pltpu.make_async_copy(kn_buf, kc_out.at[pl.ds(write_at, chunk_len)], out_sems.at[k]),
                  pltpu.make_async_copy(vn_buf, vc_out.at[pl.ds(write_at, chunk_len)], out_sems.at[k + 1])]
    for load, _ in jobs[:2 * parts]:
        load.start()

    @pl.when(is_last)
    def _():
        for load in new_loads:
            load.start()

    for load, _ in jobs[2 * parts:]:
        load.start()
    for load, store in jobs:
        load.wait()
        store.start()
    for _, store in jobs[:2 * parts]:
        store.wait()

    @pl.when(is_last)
    def _():
        for load, store in zip(new_loads, new_stores):
            load.wait()
            store.start()
        for store in new_stores:
            store.wait()

    for _, store in jobs[2 * parts:]:
        store.wait()


def finish_call(start_pos, k_shard, v_shard, k_new, v_new, result, last_index, parts=4):
    hbm = pl.BlockSpec(memory_space=pl.ANY)
    shapes = [jax.ShapeDtypeStruct(x.shape, x.dtype) for x in (k_shard, v_shard, result)]
    return pl.pallas_call(
        functools.partial(finish_kernel, (last_index, parts)),
        out_shape=tuple(shapes),
        in_specs=[pl.BlockSpec(memory_space=pltpu.SMEM)] + [hbm] * 5,
        out_specs=(hbm, hbm, hbm),
        scratch_shapes=[pltpu.VMEM(x.shape, x.dtype) for x in (k_shard, v_shard, k_new, v_new, result)]
        + [pltpu.SemaphoreType.DMA((3 * parts + 2,)), pltpu.SemaphoreType.DMA((3 * parts + 2,))],
        compiler_params=pltpu.CompilerParams(vmem_limit_bytes=60 * 2**20),
        name="finish",
    )(start_pos, k_shard, v_shard, k_new, v_new, result)


def attend_call(start_pos, hidden, norm_gain, w_query, w_key, w_value, q_gain, k_gain, cosine, sine, k_shard, v_shard, w_out, chunk_keys, scale, z_count):
    chunk_len, model_dim = hidden.shape
    keys, kv_local, head_dim = k_shard.shape
    rb = ROW_BLOCK
    nb, hb = chunk_len // rb, rb // 2
    half_cols = model_dim // 2
    heads = w_out.shape[0] // 2
    cfg = (nb, rb, keys, chunk_keys, chunk_len, scale, z_count)
    sub = pltpu.VMEM((nb, SUBS, hb, half_cols // SUBS), F32)
    flops = 4 * 4 * chunk_len * keys * 128 + 2 * chunk_len * w_out.shape[0] * model_dim // 4
    vmem = pl.BlockSpec(memory_space=pltpu.VMEM)
    hbm = pl.BlockSpec(memory_space=pl.ANY)
    new_shape = jax.ShapeDtypeStruct((chunk_len, kv_local, head_dim), BF16)
    return pl.pallas_call(
        functools.partial(attend_kernel, cfg),
        out_shape=(jax.ShapeDtypeStruct((chunk_len, model_dim), BF16), new_shape, new_shape),
        in_specs=[pl.BlockSpec(memory_space=pltpu.SMEM), hbm, vmem, hbm, hbm, hbm, vmem, vmem, vmem, vmem, hbm, hbm, hbm],
        out_specs=(hbm, hbm, hbm),
        scratch_shapes=[
            pltpu.VMEM((chunk_len, model_dim), BF16),
            pltpu.VMEM(w_query.shape, BF16),
            pltpu.VMEM((model_dim, 2 * w_key.shape[1]), BF16),
            pltpu.VMEM(k_shard.shape, BF16),
            pltpu.VMEM(k_shard.shape, BF16),
            pltpu.VMEM((kv_local, keys, head_dim), BF16),
            pltpu.VMEM((kv_local, keys, head_dim), BF16),
            pltpu.VMEM((2, chunk_len, kv_local, head_dim), BF16),
            pltpu.VMEM((kv_local, 2 * rb, head_dim), BF16),
            pltpu.VMEM((1, keys), F32),
            pltpu.VMEM((w_out.shape[0], half_cols), BF16),
            pltpu.VMEM((chunk_len, model_dim), BF16),
            pltpu.VMEM((2 * rb, 1), F32),
            pltpu.VMEM((2 * rb, 1), F32),
            pltpu.VMEM((2 * rb, 128), F32),
            pltpu.VMEM((nb, rb + STAT_ROWS, heads), F32),
            pltpu.VMEM((nb, rb + STAT_ROWS, heads), F32),
            pltpu.VMEM((rb, heads), F32),
            pltpu.VMEM((rb, 128), F32),
            pltpu.VMEM((rb, heads), F32),
            pltpu.VMEM((rb, 128), F32),
            pltpu.VMEM((nb, hb + STAT_ROWS, heads), F32),
            pltpu.VMEM((nb, hb + STAT_ROWS, heads), F32),
            pltpu.VMEM((nb, hb, heads), F32),
            pltpu.VMEM((nb, hb, 128), F32),
            pltpu.VMEM((nb, hb, heads), BF16),
            pltpu.VMEM((nb, hb, heads), F32),
            pltpu.VMEM((nb, hb, heads), F32),
            sub, sub, sub, sub, sub, sub, sub, sub,
            pltpu.SemaphoreType.DMA((3, nb)),
            pltpu.SemaphoreType.DMA((3, nb)),
            pltpu.SemaphoreType.DMA((6, nb, SUBS)),
            pltpu.SemaphoreType.DMA((6, nb, SUBS)),
            pltpu.SemaphoreType.DMA((2, 2)),
            pltpu.SemaphoreType.DMA((4,)),
            pltpu.SemaphoreType.DMA((nb,)),
            pltpu.SemaphoreType.DMA((2,)),
            pltpu.SemaphoreType.DMA((nb,)),
        ],
        compiler_params=pltpu.CompilerParams(collective_id=0, has_side_effects=True, vmem_limit_bytes=62 * 2**20),
        cost_estimate=pl.CostEstimate(flops=flops, bytes_accessed=16 * 2**20, transcendentals=4 * chunk_len * keys),
        name="attend",
    )(start_pos, hidden, norm_gain[None, :], w_query, w_key, w_value, q_gain[None, :], k_gain[None, :], cosine, sine, k_shard, v_shard, w_out)


def solution(mesh, chunk_keys=1024):
    cache_spec = P(("dp", "sp"), "tp", None)
    in_specs = (P("dp", None), P("dp"), cache_spec, cache_spec, P(None), P(None, "tp"), P(None, "tp"), P(None, "tp"), P(None), P(None), P("tp", None))
    out_specs = (P("dp", None), cache_spec, cache_spec)

    def local_step(hidden, start_pos, k_shard, v_shard, norm_gain, w_query, w_key, w_value, q_gain, k_gain, w_out):
        chunk_len, model_dim = hidden.shape
        shard_len, kv_local, head_dim = k_shard.shape
        positions = start_pos[0] + jnp.arange(chunk_len, dtype=jnp.int32)
        cosine, sine = rotary_tables(positions, head_dim)
        scale = LOG2E * head_dim ** -0.5
        result, k_new, v_new = attend_call(start_pos, hidden, norm_gain, w_query, w_key, w_value, q_gain, k_gain, cosine, sine, k_shard, v_shard, w_out,
                                           chunk_keys, scale, mesh.shape["tp"])
        k_upd, v_upd, out = finish_call(start_pos, k_shard, v_shard, k_new, v_new, result, LAST_SHARD)
        return out, k_upd, v_upd

    return jax.shard_map(local_step, mesh=mesh, in_specs=in_specs, out_specs=out_specs, check_vma=False)
```

time: 120 us -> 111 us (0.925)
  local copies, waits for them, and re-layouts: 10.3 us -> 0.08 us
    unnamed x13 -> x0, local copies, waits for them, and re-layouts: 10.2 us -> none
where the time goes in v3:
time: 111 us; the launch traced here: 110 us
  Pallas kernels  106 us (95%)
  other arithmetic  3.08 us (3%)
  between operations  1.3 us (1%)
    pallas_call x1, Pallas kernels, attend_call(): pl.pallas_call(functools.partial(attend_kernel, cfg), out_shape=(jax.Shap...  99 us
    pallas_call x1, Pallas kernels, finish_call(): pl.pallas_call(functools.partial(finish_kernel, (last_index, parts)), out...  6.57 us
    mul x1, other arithmetic, rotary_tables(): jnp.where(lane < half_dim, -1.0, 1.0)[None, :] * jnp.sin(angles)  3.06 us

profile of v3, /device:TPU:0, one launch (start us, length us, event | category | flops | bytes accessed | tf_op | source)
XLA Modules:
  0.0 110.0 jit_solution(7630730266100128422)
XLA Ops:
  1.3 0.1 mul.27
  1.4 3.1 %fusion = (f32[1024,128]{1,0:T(8,128)}, f32[1024,128]{1,0:T(8,128)}) fusion(f32[128]{0:T(128)S(1)} %compare_select_fusion, f32[128]{0:T(128)S(1)} %mul.27, f32[1024]{0:T(1024)S(1)} %add_convert_fusion), kind=kLoop, calls=%fused_computation.2 | loop fusion | flops 262144 | bytes 1053696 | tf_op jit(solution)/shard_map/mul | solution.py:30
  4.5 99.0 %attend.1 = (bf16[1024,2048]{1,0:T(8,128)(2,1)}, bf16[1024,2,128]{2,1,0:T(2,128)(2,1)}, bf16[1024,2,128]{2,1,0:T(2,128)(2,1)}) custom-call(s32[1]{0:T(128)} %copy.14.pos_ref, bf16[1024,2048]{1,0:T(8,128)(2,1)} %h_hbm.1, f32[1,2048]{1,0:T(1,128)} %bitcast.5, bf16[2048,512]{1,0:T(8,128)(2,1)} %wq_hbm.1, bf16[2048,256]{1,0:T(8,128)(2,1)} %wk_hbm.1, ...), custom_call_target="tpu_custom_call" | custom-call | flops 9126805504 | bytes 16777216 | tf_op jit(solution)/shard_map/attend/pallas_call | solution.py:495
  103.5 6.6 %finish.1 = (bf16[4096,2,128]{2,1,0:T(2,128)(2,1)}, bf16[4096,2,128]{2,1,0:T(2,128)(2,1)}, bf16[1024,2048]{1,0:T(8,128)(2,1)}) custom-call(s32[1]{0:T(128)} %copy.14.pos_ref, bf16[4096,2,128]{2,1,0:T(2,128)(2,1)} %kc_hbm.3, bf16[4096,2,128]{2,1,0:T(2,128)(2,1)} %vc_hbm.3, bf16[1024,2,128]{2,1,0:T(2,128)(2,1)} %get-tuple-element.9.kn_hbm, ...), custom_call_target="tpu_custom_call" | custom-call | tf_op jit(solution)/shard_map/finish/pallas_call | solution.py:470
  (4 shorter events, 0.0 us)

commit v4 on v3

--- a/solution.py
+++ b/solution.py
@@ -16,18 +16,24 @@
 ROW_BLOCK = 128
 STAT_ROWS = 8
 SUBS = 4
+PIECE_STEPS = SUBS // 4
 LAG_Y = 6
 LAG_PROJECT = 7
-LAG_HOP = 3
+LAG_P = 3
+LAG_M = 3
+LAG_F = 3
+LAG_YF = 3
 LAST_SHARD = 3
-
-
-def rotary_tables(positions, head_dim):
+ATTEND_VMEM = 50
+
+
+def rotary_tables(first_pos, chunk_len, head_dim):
     half_dim = head_dim // 2
     inv_freq = ROPE_BASE ** (-2.0 * jnp.arange(half_dim, dtype=jnp.float32) / head_dim)
-    lane = jnp.arange(head_dim)
-    angles = positions.astype(jnp.float32)[:, None] * jnp.tile(inv_freq, 2)[None, :]
-    return jnp.cos(angles), jnp.where(lane < half_dim, -1.0, 1.0)[None, :] * jnp.sin(angles)
+    starts = first_pos + ROW_BLOCK * jnp.arange(chunk_len // ROW_BLOCK, dtype=jnp.int32)
+    places = jnp.concatenate([starts, jnp.arange(ROW_BLOCK, dtype=jnp.int32)])
+    angles = places.astype(jnp.float32)[:, None] * jnp.tile(inv_freq, 2)[None, :]
+    return jnp.cos(angles), jnp.sin(angles)
 
 
 def stats_tile(rows, columns):
@@ -59,11 +65,11 @@
     return nums, columns
 
 
-def attend_kernel(cfg, pos_ref, h_hbm, gain_ref, wq_hbm, wk_hbm, wv_hbm, qg_ref, kg_ref, cos_ref, sin_ref, kc_hbm, vc_hbm, w_hbm, out_hbm, kn_hbm, vn_hbm,
-                  h_buf, wq_buf, wkv_buf, kc_buf, vc_buf, k_buf, v_buf, new_buf, q_buf, bias_ref, w_buf, out_buf, att_m, att_l, att_acc,
+def attend_kernel(cfg, pos_ref, h_hbm, gain_ref, wq_hbm, wk_hbm, wv_hbm, qg_ref, kg_ref, cos_ref, sin_ref, kc_hbm, vc_hbm, w_hbm, out_buf, kc_buf, vc_buf, new_buf,
+                  h_buf, wq_buf, wkv_buf, k_buf, v_buf, q_buf, bias_ref, w_buf, att_m, att_l, att_acc,
                   a_send, a_recv, own_num, own_st, comb_num, comb_st, y_send, y_recv, y_num, y_st, o_own, o_send, o_recv,
                   p_buf, p_recv, m_send, m_recv, f_buf, yf_recv, d1_recv, d2_recv, row_send, row_recv, sub_send, sub_recv,
-                  kv_sems, w_sems, h_sems, new_sems, out_sems):
+                  kv_sems, w_sems, h_sems):
     nb, rb, keys, chunk_keys, chunk_len, scale, z_count = cfg
     hb = rb // 2
     dp, z, sp = lax.axis_index("dp"), lax.axis_index("tp"), lax.axis_index("sp")
@@ -105,8 +111,6 @@
     wk_load = pltpu.make_async_copy(wk_hbm, wkv_buf.at[:, pl.ds(0, kv_cols)], w_sems.at[1])
     wv_load = pltpu.make_async_copy(wv_hbm, wkv_buf.at[:, pl.ds(kv_cols, kv_cols)], w_sems.at[2])
     w_load = pltpu.make_async_copy(w_hbm.at[:, my_cols], w_buf, w_sems.at[3])
-    kn_store = pltpu.make_async_copy(new_buf.at[0], kn_hbm, new_sems.at[0])
-    vn_store = pltpu.make_async_copy(new_buf.at[1], vn_hbm, new_sems.at[1])
 
     @pl.when(last)
     def _():
@@ -142,8 +146,15 @@
     def normalize(x, gain):
         return x * lax.rsqrt(jnp.mean(x * x, axis=-1, keepdims=True) + NORM_EPS) * gain
 
-    def rotate(x, span):
-        return (x * cos_ref[span, :] + pltpu.roll(x, 64, 1) * sin_ref[span, :]).astype(BF16)
+    def block_angles(b):
+        cos_a, sin_a = cos_ref[pl.ds(b, 1), :], sin_ref[pl.ds(b, 1), :]
+        cos_b, sin_b = cos_ref[nb:nb + rb, :], sin_ref[nb:nb + rb, :]
+        lane = lax.broadcasted_iota(jnp.int32, (rb, 128), 1)
+        sine = sin_a * cos_b + cos_a * sin_b
+        return cos_a * cos_b - sin_a * sin_b, jnp.where(lane < 64, -sine, sine)
+
+    def rotate(x, angles):
+        return (x * angles[0] + pltpu.roll(x, 64, 1) * angles[1]).astype(BF16)
 
     def project_q(b):
         @pl.when(jnp.logical_not(last))
@@ -157,25 +168,26 @@
         span = block_rows(b, rb)
         normed = normalize(h_buf[span, :].astype(F32), gain_ref[...]).astype(BF16)
         proj = jnp.dot(normed, wq_buf[...], preferred_element_type=F32)
+        angles = block_angles(b)
         for head in range(4):
-            q_buf[head // 2, (head % 2) * rb:(head % 2 + 1) * rb, :] = rotate(normalize(proj[:, head * 128:(head + 1) * 128], qg_ref[...]), span)
-
-    def project_new(part, carry):
+            q_buf[head // 2, (head % 2) * rb:(head % 2 + 1) * rb, :] = rotate(normalize(proj[:, head * 128:(head + 1) * 128], qg_ref[...]), angles)
+
+    def project_new(part):
         rows = 2 * rb
         for b in range(2):
             h_load(2 * part + b).wait()
         span = block_rows(part, rows)
         normed = normalize(h_buf[span, :].astype(F32), gain_ref[...]).astype(BF16)
         proj = jnp.dot(normed, wkv_buf[...], preferred_element_type=F32)
+        angles = [jnp.concatenate(pair, axis=0) for pair in zip(block_angles(2 * part), block_angles(2 * part + 1))]
         place = pl.ds(pl.multiple_of(old_len + part * rows, rows), rows)
         heads = []
         for n in range(2):
-            heads.append(rotate(normalize(proj[:, n * 128:(n + 1) * 128], kg_ref[...]), span))
+            heads.append(rotate(normalize(proj[:, n * 128:(n + 1) * 128], kg_ref[...]), angles))
             k_buf[n, place, :] = heads[n]
             v_buf[n, place, :] = proj[:, kv_cols + n * 128:kv_cols + (n + 1) * 128].astype(BF16)
         new_buf[0, span] = jnp.concatenate(heads, axis=1).reshape(rows, 2, 128)
         new_buf[1, span] = proj[:, kv_cols:].astype(BF16).reshape(rows, 2, 128)
-        return carry
 
     def split_heads(start, stop):
         for src, dst in ((kc_buf, k_buf), (vc_buf, v_buf)):
@@ -200,15 +212,15 @@
     def _():
         wk_load.wait()
         wv_load.wait()
-        lax.fori_loop(0, chunk_len // (2 * rb), project_new, 0)
-        kn_store.start()
-        vn_store.start()
+        for n in range(2):
+            k_buf[n, old_len:keys, :] = jnp.zeros((chunk_len, 128), BF16)
+            v_buf[n, old_len:keys, :] = jnp.zeros((chunk_len, 128), BF16)
 
     def row_copy(kind, b, src, dst, peer):
         return pltpu.make_async_remote_copy(src.at[b], dst.at[b], row_send.at[kind, b], row_recv.at[kind, b], device_id=peer, device_id_type=MESH)
 
     def sub_copy(kind, b, j, src, dst, peer):
-        return pltpu.make_async_remote_copy(src.at[b, j], dst.at[b, j], sub_send.at[kind, b, j], sub_recv.at[kind, b, j], device_id=peer, device_id_type=MESH)
+        return pltpu.make_async_remote_copy(src.at[b, j], dst.at[b, j], sub_send.at[kind, b], sub_recv.at[kind, b, j], device_id=peer, device_id_type=MESH)
 
     copy_a = lambda b: row_copy(0, b, a_send, a_recv, core_peer)
     copy_y = lambda b: row_copy(1, b, y_send, y_recv, y_peer)
@@ -220,9 +232,8 @@
     copy_d1 = lambda b, j: sub_copy(4, b, j, f_buf, d1_recv, core_peer)
     copy_d2 = lambda b, j: sub_copy(5, b, j, yf_recv, d2_recv, core_peer)
 
-    def out_store(b):
-        rows = pl.ds(pl.multiple_of(b * rb, rb), rb)
-        return pltpu.make_async_copy(out_buf.at[rows], out_hbm.at[rows], out_sems.at[b])
+    def sub_sent(kind, b, src, dst, peer):
+        pltpu.make_async_remote_copy(src.at[b], dst.at[b], sub_send.at[kind, b], sub_recv.at[kind, b, 0], device_id=peer, device_id_type=MESH).wait_send()
 
     def columns_of(core, j):
         return pl.ds(pl.multiple_of(core * half_cols + j * sub_cols, sub_cols), sub_cols)
@@ -259,6 +270,10 @@
         n = c if head else other_c
 
         if piece == 0:
+            @pl.when(jnp.logical_and(last, lax.rem(b, 2) == 0))
+            def _():
+                project_new(lax.div(b, 2))
+
             project_q(b)
         if head == 0:
             @pl.when(b == 0)
@@ -356,27 +371,22 @@
         out_buf[half_rows(b, y), columns_of(other_c, j)] = d1_recv[b, j].astype(BF16)
         copy_d2(b, j).wait_recv()
         out_buf[half_rows(b, other_y), columns_of(other_c, j)] = d2_recv[b, j].astype(BF16)
-        if j == SUBS - 1:
-            out_store(b).start()
 
     def stage_sent(b):
         for sent in (copy_a, copy_y, copy_o):
             sent(b).wait_send()
-        out_store(b).wait()
-        for j in range(SUBS):
-            for sent in (copy_yf, copy_d1, copy_d2):
-                sent(b, j).wait_send()
+        sub_sent(3, b, f_buf, yf_recv, y_peer)
+        sub_sent(4, b, f_buf, d1_recv, core_peer)
+        sub_sent(5, b, yf_recv, d2_recv, core_peer)
 
         @pl.when(is_mid)
         def _():
-            for j in range(SUBS):
-                copy_m(b, j).wait_send()
-                copy_f(b, j).wait_send()
+            sub_sent(1, b, m_send, m_recv, cross_peer)
+            sub_sent(2, b, f_buf, f_buf, pair_peer)
 
         @pl.when(is_end)
         def _():
-            for j in range(SUBS):
-                copy_p(b, j).wait_send()
+            sub_sent(0, b, p_buf, p_recv, pair_peer)
 
     def run(stage, it, step, lag, guard=None, sub=True):
         j = (step - lag) % SUBS
@@ -394,19 +404,22 @@
             else:
                 stage(b)
 
-    lag_p, hop = LAG_PROJECT + LAG_HOP, LAG_HOP
-    lag_store = lag_p + 3 * hop + 2
+    lag_p = LAG_PROJECT + LAG_P
+    lag_m = lag_p + LAG_M
+    lag_f = lag_m + LAG_F
+    lag_store = lag_f + LAG_YF + 2
 
     def body(it, carry):
         for step in range(SUBS):
             run(stage_store, it, step, lag_store)
-            run(stage_y_total, it, step, lag_p + 3 * hop, is_end)
-            run(stage_end_total, it, step, lag_p + 2 * hop, is_end)
-            run(stage_y_total, it, step, lag_p + 2 * hop, is_mid)
-            run(stage_total, it, step, lag_p + hop, is_mid)
+            run(stage_y_total, it, step, lag_f + LAG_YF, is_end)
+            run(stage_end_total, it, step, lag_f, is_end)
+            run(stage_y_total, it, step, lag_m + LAG_YF, is_mid)
+            run(stage_total, it, step, lag_m, is_mid)
             run(stage_pair_sum, it, step, lag_p, is_mid)
-            run(stage_attend, it, step, 0)
-            run(stage_core_merge, it, step, SUBS - 1, sub=False)
+            if step % PIECE_STEPS == 0:
+                run(lambda b, j: stage_attend(b, j // PIECE_STEPS), it, step, 0)
+            run(stage_core_merge, it, step, 3 * PIECE_STEPS, sub=False)
             run(stage_y_merge, it, step, LAG_Y, sub=False)
             run(stage_project, it, step, LAG_PROJECT, sub=False)
         return carry
@@ -414,69 +427,45 @@
     lax.fori_loop(0, nb + (lag_store + SUBS - 1) // SUBS, body, 0)
     lax.fori_loop(0, nb, lambda b, carry: (stage_sent(b), carry)[1], 0)
 
-    @pl.when(last)
-    def _():
-        kn_store.wait()
-        vn_store.wait()
-
-
-def finish_kernel(cfg, pos_ref, kc_hbm, vc_hbm, kn_hbm, vn_hbm, x_hbm, kc_out, vc_out, x_out, kc_buf, vc_buf, kn_buf, vn_buf, x_buf, in_sems, out_sems):
-    last_index, parts = cfg
-    is_last = lax.axis_index("sp") == last_index
-    shard_len, chunk_len = kc_buf.shape[0], kn_buf.shape[0]
-    write_at = jnp.clip(pos_ref[0] - last_index * shard_len, 0, shard_len - chunk_len)
-    jobs = []
-    for src, buf, dst in ((kc_hbm, kc_buf, kc_out), (vc_hbm, vc_buf, vc_out), (x_hbm, x_buf, x_out)):
-        rows = buf.shape[0] // parts
-        for part in range(parts):
-            span = pl.ds(part * rows, rows)
-            k = len(jobs)
-            jobs.append((pltpu.make_async_copy(src.at[span], buf.at[span], in_sems.at[k]), pltpu.make_async_copy(buf.at[span], dst.at[span], out_sems.at[k])))
-    k = len(jobs)
-    new_loads = [pltpu.make_async_copy(kn_hbm, kn_buf, in_sems.at[k]), pltpu.make_async_copy(vn_hbm, vn_buf, in_sems.at[k + 1])]
-    new_stores = [pltpu.make_async_copy(kn_buf, kc_out.at[pl.ds(write_at, chunk_len)], out_sems.at[k]),
-                  pltpu.make_async_copy(vn_buf, vc_out.at[pl.ds(write_at, chunk_len)], out_sems.at[k + 1])]
-    for load, _ in jobs[:2 * parts]:
-        load.start()
+
+def finish_kernel(pos_ref, kc_buf, vc_buf, new_buf, x_buf, kc_out, vc_out, x_out, sems):
+    is_last = lax.axis_index("sp") == LAST_SHARD
+    shard_len, chunk_len = kc_buf.shape[0], new_buf.shape[1]
+    write_at = jnp.clip(pos_ref[0] - LAST_SHARD * shard_len, 0, shard_len - chunk_len)
+    span = pl.ds(write_at, chunk_len)
+    k_store = pltpu.make_async_copy(kc_buf, kc_out, sems.at[0])
+    v_store = pltpu.make_async_copy(vc_buf, vc_out, sems.at[1])
+    x_store = pltpu.make_async_copy(x_buf, x_out, sems.at[2])
+    new_stores = (pltpu.make_async_copy(new_buf.at[0], kc_out.at[span], sems.at[3]), pltpu.make_async_copy(new_buf.at[1], vc_out.at[span], sems.at[4]))
+    k_store.start()
+    v_store.start()
+    x_store.start()
+    k_store.wait()
+    v_store.wait()
 
     @pl.when(is_last)
     def _():
-        for load in new_loads:
-            load.start()
-
-    for load, _ in jobs[2 * parts:]:
-        load.start()
-    for load, store in jobs:
-        load.wait()
-        store.start()
-    for _, store in jobs[:2 * parts]:
-        store.wait()
-
-    @pl.when(is_last)
-    def _():
-        for load, store in zip(new_loads, new_stores):
-            load.wait()
+        for store in new_stores:
             store.start()
         for store in new_stores:
             store.wait()
 
-    for _, store in jobs[2 * parts:]:
-        store.wait()
-
-
-def finish_call(start_pos, k_shard, v_shard, k_new, v_new, result, last_index, parts=4):
+    x_store.wait()
+
+
+def finish_call(start_pos, k_old, v_old, new_rows, result):
     hbm = pl.BlockSpec(memory_space=pl.ANY)
-    shapes = [jax.ShapeDtypeStruct(x.shape, x.dtype) for x in (k_shard, v_shard, result)]
+    vmem = pl.BlockSpec(memory_space=pltpu.VMEM)
+    shapes = [jax.ShapeDtypeStruct(x.shape, x.dtype) for x in (k_old, v_old, result)]
     return pl.pallas_call(
-        functools.partial(finish_kernel, (last_index, parts)),
+        finish_kernel,
         out_shape=tuple(shapes),
-        in_specs=[pl.BlockSpec(memory_space=pltpu.SMEM)] + [hbm] * 5,
+        in_specs=[pl.BlockSpec(memory_space=pltpu.SMEM)] + [vmem] * 4,
         out_specs=(hbm, hbm, hbm),
-        scratch_shapes=[pltpu.VMEM(x.shape, x.dtype) for x in (k_shard, v_shard, k_new, v_new, result)]
-        + [pltpu.SemaphoreType.DMA((3 * parts + 2,)), pltpu.SemaphoreType.DMA((3 * parts + 2,))],
-        compiler_params=pltpu.CompilerParams(vmem_limit_bytes=60 * 2**20),
+        scratch_shapes=[pltpu.SemaphoreType.DMA((5,))],
+        compiler_params=pltpu.CompilerParams(vmem_limit_bytes=2 * 2**20),
         name="finish",
-    )(start_pos, k_shard, v_shard, k_new, v_new, result)
+    )(start_pos, k_old, v_old, new_rows, result)
 
 
 def attend_call(start_pos, hidden, norm_gain, w_query, w_key, w_value, q_gain, k_gain, cosine, sine, k_shard, v_shard, w_out, chunk_keys, scale, z_count):
@@ -491,25 +480,22 @@
     flops = 4 * 4 * chunk_len * keys * 128 + 2 * chunk_len * w_out.shape[0] * model_dim // 4
     vmem = pl.BlockSpec(memory_space=pltpu.VMEM)
     hbm = pl.BlockSpec(memory_space=pl.ANY)
-    new_shape = jax.ShapeDtypeStruct((chunk_len, kv_local, head_dim), BF16)
+    outs = (pltpu.VMEM((chunk_len, model_dim), BF16), pltpu.VMEM(k_shard.shape, BF16), pltpu.VMEM(k_shard.shape, BF16),
+            pltpu.VMEM((2, chunk_len, kv_local, head_dim), BF16))
     return pl.pallas_call(
         functools.partial(attend_kernel, cfg),
-        out_shape=(jax.ShapeDtypeStruct((chunk_len, model_dim), BF16), new_shape, new_shape),
+        out_shape=outs,
         in_specs=[pl.BlockSpec(memory_space=pltpu.SMEM), hbm, vmem, hbm, hbm, hbm, vmem, vmem, vmem, vmem, hbm, hbm, hbm],
-        out_specs=(hbm, hbm, hbm),
+        out_specs=(vmem, vmem, vmem, vmem),
         scratch_shapes=[
             pltpu.VMEM((chunk_len, model_dim), BF16),
             pltpu.VMEM(w_query.shape, BF16),
             pltpu.VMEM((model_dim, 2 * w_key.shape[1]), BF16),
-            pltpu.VMEM(k_shard.shape, BF16),
-            pltpu.VMEM(k_shard.shape, BF16),
             pltpu.VMEM((kv_local, keys, head_dim), BF16),
             pltpu.VMEM((kv_local, keys, head_dim), BF16),
-            pltpu.VMEM((2, chunk_len, kv_local, head_dim), BF16),
             pltpu.VMEM((kv_local, 2 * rb, head_dim), BF16),
             pltpu.VMEM((1, keys), F32),
             pltpu.VMEM((w_out.shape[0], half_cols), BF16),
-            pltpu.VMEM((chunk_len, model_dim), BF16),
             pltpu.VMEM((2 * rb, 1), F32),
             pltpu.VMEM((2 * rb, 1), F32),
             pltpu.VMEM((2 * rb, 128), F32),
@@ -529,15 +515,13 @@
             sub, sub, sub, sub, sub, sub, sub, sub,
             pltpu.SemaphoreType.DMA((3, nb)),
             pltpu.SemaphoreType.DMA((3, nb)),
-            pltpu.SemaphoreType.DMA((6, nb, SUBS)),
+            pltpu.SemaphoreType.DMA((6, nb)),
             pltpu.SemaphoreType.DMA((6, nb, SUBS)),
             pltpu.SemaphoreType.DMA((2, 2)),
             pltpu.SemaphoreType.DMA((4,)),
             pltpu.SemaphoreType.DMA((nb,)),
-            pltpu.SemaphoreType.DMA((2,)),
-            pltpu.SemaphoreType.DMA((nb,)),
         ],
-        compiler_params=pltpu.CompilerParams(collective_id=0, has_side_effects=True, vmem_limit_bytes=62 * 2**20),
+        compiler_params=pltpu.CompilerParams(collective_id=0, has_side_effects=True, vmem_limit_bytes=ATTEND_VMEM * 2**20),
         cost_estimate=pl.CostEstimate(flops=flops, bytes_accessed=16 * 2**20, transcendentals=4 * chunk_len * keys),
         name="attend",
     )(start_pos, hidden, norm_gain[None, :], w_query, w_key, w_value, q_gain[None, :], k_gain[None, :], cosine, sine, k_shard, v_shard, w_out)
@@ -551,12 +535,11 @@
     def local_step(hidden, start_pos, k_shard, v_shard, norm_gain, w_query, w_key, w_value, q_gain, k_gain, w_out):
         chunk_len, model_dim = hidden.shape
         shard_len, kv_local, head_dim = k_shard.shape
-        positions = start_pos[0] + jnp.arange(chunk_len, dtype=jnp.int32)
-        cosine, sine = rotary_tables(positions, head_dim)
+        cosine, sine = rotary_tables(start_pos[0], chunk_len, head_dim)
         scale = LOG2E * head_dim ** -0.5
-        result, k_new, v_new = attend_call(start_pos, hidden, norm_gain, w_query, w_key, w_value, q_gain, k_gain, cosine, sine, k_shard, v_shard, w_out,
+        result, k_old, v_old, new_rows = attend_call(start_pos, hidden, norm_gain, w_query, w_key, w_value, q_gain, k_gain, cosine, sine, k_shard, v_shard, w_out,
                                            chunk_keys, scale, mesh.shape["tp"])
-        k_upd, v_upd, out = finish_call(start_pos, k_shard, v_shard, k_new, v_new, result, LAST_SHARD)
+        k_upd, v_upd, out = finish_call(start_pos, k_old, v_old, new_rows, result)
         return out, k_upd, v_upd
 
     return jax.shard_map(local_step, mesh=mesh, in_specs=in_specs, out_specs=out_specs, check_vma=False)

time: 111 us -> 102 us (0.919); the launches traced: 110 us -> 102 us
  Pallas kernels: 106 us -> 99.7 us
  other arithmetic: 3.08 us -> 1.08 us
    pallas_call x2, Pallas kernels: 106 us -> 99.7 us  [the longest x1 96.3 us: attend_call(): pl.pallas_call(functools.partial(attend_kernel, cfg), out_shape=outs, in_...]
    mul x1 -> x0, other arithmetic: 3.06 us -> none  [rotary_tables(): jnp.where(lane < half_dim, -1.0, 1.0)[None, :] * jnp.sin(angles)]
where the time goes in v4:
time: 102 us
  Pallas kernels  99.7 us (98%)
  between operations  1.31 us (1%)
  other arithmetic  1.08 us (1%)
    pallas_call x1, Pallas kernels, attend_call(): pl.pallas_call(functools.partial(attend_kernel, cfg), out_shape=outs, in_...  96.3 us
    pallas_call x1, Pallas kernels, finish_call(): pl.pallas_call(finish_kernel, out_shape=tuple(shapes), in_specs=[pl.Block...  3.44 us

profile of v4, /device:TPU:0, one launch (start us, length us, event | category | flops | bytes accessed | tf_op | source)
XLA Modules:
  0.0 102.2 jit_solution(5643130681659773224)
XLA Ops:
  1.3 0.1 mul.25
  1.4 0.1 add_convert_fusion
  1.5 1.0 multiply_sine_fusion
  2.5 96.3 %attend.1 = (bf16[1024,2048]{1,0:T(8,128)(2,1)S(1)}, bf16[4096,2,128]{2,1,0:T(2,128)(2,1)S(1)}, bf16[4096,2,128]{2,1,0:T(2,128)(2,1)S(1)}, bf16[2,1024,2,128]{3,2,1,0:T(2,128)(2,1)S(1)}) custom-call(s32[1]{0:T(128)} %copy.14.pos_ref, bf16[1024,2048]{1,0:T(8,128)(2,1)} %h_hbm.1, f32[1,2048]{1,0:T(1,128)} %bitcast.5, bf16[2048,512]{1,0:T(8,128)(2,1)} %wq_hbm.1, ...), custom_call_target="tpu_custom_call" | custom-call | flops 9126805504 | bytes 16777216 | tf_op jit(solution)/shard_map/attend/pallas_call | solution.py:485
  98.8 3.4 %finish.1 = (bf16[4096,2,128]{2,1,0:T(2,128)(2,1)}, bf16[4096,2,128]{2,1,0:T(2,128)(2,1)}, bf16[1024,2048]{1,0:T(8,128)(2,1)}) custom-call(s32[1]{0:T(128)} %copy.14.pos_ref, bf16[4096,2,128]{2,1,0:T(2,128)(2,1)S(1)} %get-tuple-element.10.kc_buf, bf16[4096,2,128]{2,1,0:T(2,128)(2,1)S(1)} %get-tuple-element.11.vc_buf, ...), custom_call_target="tpu_custom_call" | custom-call | tf_op jit(solution)/shard_map/finish/pallas_call | solution.py:460
  (4 shorter events, 0.0 us)

commit v5 on v4

--- a/solution.py
+++ b/solution.py
@@ -238,10 +238,10 @@
     def columns_of(core, j):
         return pl.ds(pl.multiple_of(core * half_cols + j * sub_cols, sub_cols), sub_cols)
 
-    def attend(b, n, half):
+    def attend(b, n, half, width):
         q = q_buf[n]
         row = b * rb + lax.rem(lax.broadcasted_iota(jnp.int32, (2 * rb, 1), 0), rb) + jnp.where(last, 0, keys)
-        first, width = half * (keys // 2), keys // 2
+        first = half * (keys // 2)
         scores = lax.dot_general(q, k_buf[n, first:first + width, :], (((1,), (1,)), ((), ())), preferred_element_type=F32)
         parts = []
         for start in range(0, width, chunk_keys):
@@ -265,24 +265,8 @@
             att_m[...], att_l[...], att_acc[...] = m, l, acc
         return acc, m, l
 
-    def stage_attend(b, piece):
-        head, half = piece // 2, piece % 2
-        n = c if head else other_c
-
-        if piece == 0:
-            @pl.when(jnp.logical_and(last, lax.rem(b, 2) == 0))
-            def _():
-                project_new(lax.div(b, 2))
-
-            project_q(b)
-        if head == 0:
-            @pl.when(b == 0)
-            def _():
-                prepare_keys(half)
-
-        acc, m, l = attend(b, n, half)
-        if not half:
-            return
+    def keep_piece(b, n, head, width):
+        acc, m, l = attend(b, n, 1, width)
         tile = stats_tile(rb, [m[:rb], l[:rb], m[rb:], l[rb:]])
         if head:
             own_num[:, 0:128] = acc[:rb]
@@ -291,14 +275,41 @@
         else:
             a_send[b, :rb, 0:128] = acc[:rb]
             a_send[b, :rb, 128:256] = acc[rb:]
-            rows8 = stats_rows(tile)
-            a_send[b, rb:rb + STAT_ROWS, :] = jnp.concatenate([rows8, rows8], axis=1)
+            a_send[b, :, 256:384] = tile
             copy_a(b).start()
+
+    def stage_attend(b, piece):
+        head, half = piece // 2, piece % 2
+        n = c if head else other_c
+
+        if piece == 0:
+            @pl.when(jnp.logical_and(last, lax.rem(b, 2) == 0))
+            def _():
+                project_new(lax.div(b, 2))
+
+            project_q(b)
+        if head == 0:
+            @pl.when(b == 0)
+            def _():
+                prepare_keys(half)
+
+        if not half:
+            attend(b, n, half, keys // 2)
+            return
+
+        short = jnp.logical_and(last, b < nb // 2)
+
+        @pl.when(short)
+        def _():
+            keep_piece(b, n, head, keys // 2 - chunk_len // 2)
+
+        @pl.when(jnp.logical_not(short))
+        def _():
+            keep_piece(b, n, head, keys // 2)
 
     def stage_core_merge(b):
         copy_a(b).wait_recv()
-        peer_tile = stats_columns(a_recv[b, rb:rb + STAT_ROWS, 0:128])
-        nums, columns = merge(own_num[...], own_st[...], a_recv[b, :rb, :], peer_tile, scale)
+        nums, columns = merge(own_num[...], own_st[...], a_recv[b, :, 0:256], a_recv[b, :, 256:384], scale)
         tile = stats_tile(rb, columns)
         comb_num[:, 0:128] = nums[0]
         comb_num[:, 128:256] = nums[1]
@@ -499,8 +510,8 @@
             pltpu.VMEM((2 * rb, 1), F32),
             pltpu.VMEM((2 * rb, 1), F32),
             pltpu.VMEM((2 * rb, 128), F32),
-            pltpu.VMEM((nb, rb + STAT_ROWS, heads), F32),
-            pltpu.VMEM((nb, rb + STAT_ROWS, heads), F32),
+            pltpu.VMEM((nb, rb, heads + 128), F32),
+            pltpu.VMEM((nb, rb, heads + 128), F32),
             pltpu.VMEM((rb, heads), F32),
             pltpu.VMEM((rb, 128), F32),
             pltpu.VMEM((rb, heads), F32),
@@ -527,7 +538,7 @@
     )(start_pos, hidden, norm_gain[None, :], w_query, w_key, w_value, q_gain[None, :], k_gain[None, :], cosine, sine, k_shard, v_shard, w_out)
 
 
-def solution(mesh, chunk_keys=1024):
+def solution(mesh, chunk_keys=512):
     cache_spec = P(("dp", "sp"), "tp", None)
     in_specs = (P("dp", None), P("dp"), cache_spec, cache_spec, P(None), P(None, "tp"), P(None, "tp"), P(None, "tp"), P(None), P(None), P("tp", None))
     out_specs = (P("dp", None), cache_spec, cache_spec)

time: 102 us -> 101 us (level)
  no operation moved by 1% of the time
where the time goes in v5:
time: 101 us
  Pallas kernels  98.8 us (98%)
  between operations  1.31 us (1%)
  other arithmetic  1.08 us (1%)
    pallas_call x1, Pallas kernels, attend_call(): pl.pallas_call(functools.partial(attend_kernel, cfg), out_shape=outs, in_...  95.3 us
    pallas_call x1, Pallas kernels, finish_call(): pl.pallas_call(finish_kernel, out_shape=tuple(shapes), in_specs=[pl.Block...  3.44 us

profile of v5, /device:TPU:0, one launch (start us, length us, event | category | flops | bytes accessed | tf_op | source)
XLA Modules:
  0.0 101.2 jit_solution(5384533296821691796)
XLA Ops:
  1.3 0.1 mul.25
  1.4 0.1 add_convert_fusion
  1.5 1.0 multiply_sine_fusion
  2.5 95.3 %attend.1 = (bf16[1024,2048]{1,0:T(8,128)(2,1)S(1)}, bf16[4096,2,128]{2,1,0:T(2,128)(2,1)S(1)}, bf16[4096,2,128]{2,1,0:T(2,128)(2,1)S(1)}, bf16[2,1024,2,128]{3,2,1,0:T(2,128)(2,1)S(1)}) custom-call(s32[1]{0:T(128)} %copy.14.pos_ref, bf16[1024,2048]{1,0:T(8,128)(2,1)} %h_hbm.1, f32[1,2048]{1,0:T(1,128)} %bitcast.5, bf16[2048,512]{1,0:T(8,128)(2,1)} %wq_hbm.1, ...), custom_call_target="tpu_custom_call" | custom-call | flops 9126805504 | bytes 16777216 | tf_op jit(solution)/shard_map/attend/pallas_call | solution.py:496
  97.8 3.4 %finish.1 = (bf16[4096,2,128]{2,1,0:T(2,128)(2,1)}, bf16[4096,2,128]{2,1,0:T(2,128)(2,1)}, bf16[1024,2048]{1,0:T(8,128)(2,1)}) custom-call(s32[1]{0:T(128)} %copy.14.pos_ref, bf16[4096,2,128]{2,1,0:T(2,128)(2,1)S(1)} %get-tuple-element.10.kc_buf, bf16[4096,2,128]{2,1,0:T(2,128)(2,1)S(1)} %get-tuple-element.11.vc_buf, ...), custom_call_target="tpu_custom_call" | custom-call | tf_op jit(solution)/shard_map/finish/pallas_call | solution.py:471
  (4 shorter events, 0.0 us)

commit v6 on v5

--- a/solution.py
+++ b/solution.py
@@ -22,7 +22,7 @@
 LAG_P = 3
 LAG_M = 3
 LAG_F = 3
-LAG_YF = 3
+LAG_YF = 4
 LAST_SHARD = 3
 ATTEND_VMEM = 50
 
@@ -428,10 +428,10 @@
             run(stage_y_total, it, step, lag_m + LAG_YF, is_mid)
             run(stage_total, it, step, lag_m, is_mid)
             run(stage_pair_sum, it, step, lag_p, is_mid)
+            run(stage_y_merge, it, step, LAG_Y, sub=False)
             if step % PIECE_STEPS == 0:
                 run(lambda b, j: stage_attend(b, j // PIECE_STEPS), it, step, 0)
             run(stage_core_merge, it, step, 3 * PIECE_STEPS, sub=False)
-            run(stage_y_merge, it, step, LAG_Y, sub=False)
             run(stage_project, it, step, LAG_PROJECT, sub=False)
         return carry
 

time: 101 us -> 101 us (level)
  no operation moved by 1% of the time
where the time goes in v6:
time: 101 us
  Pallas kernels  98.4 us (97%)
  between operations  1.31 us (1%)
  other arithmetic  1.08 us (1%)
    pallas_call x1, Pallas kernels, attend_call(): pl.pallas_call(functools.partial(attend_kernel, cfg), out_shape=outs, in_...  94.9 us
    pallas_call x1, Pallas kernels, finish_call(): pl.pallas_call(finish_kernel, out_shape=tuple(shapes), in_specs=[pl.Block...  3.44 us

profile of v6, /device:TPU:0, one launch (start us, length us, event | category | flops | bytes accessed | tf_op | source)
XLA Modules:
  0.0 100.8 jit_solution(17220341378879175386)
XLA Ops:
  1.3 0.1 mul.25
  1.4 0.1 add_convert_fusion
  1.5 1.0 multiply_sine_fusion
  2.5 94.9 %attend.1 = (bf16[1024,2048]{1,0:T(8,128)(2,1)S(1)}, bf16[4096,2,128]{2,1,0:T(2,128)(2,1)S(1)}, bf16[4096,2,128]{2,1,0:T(2,128)(2,1)S(1)}, bf16[2,1024,2,128]{3,2,1,0:T(2,128)(2,1)S(1)}) custom-call(s32[1]{0:T(128)} %copy.14.pos_ref, bf16[1024,2048]{1,0:T(8,128)(2,1)} %h_hbm.1, f32[1,2048]{1,0:T(1,128)} %bitcast.5, bf16[2048,512]{1,0:T(8,128)(2,1)} %wq_hbm.1, ...), custom_call_target="tpu_custom_call" | custom-call | flops 9126805504 | bytes 16777216 | tf_op jit(solution)/shard_map/attend/pallas_call | solution.py:496
  97.4 3.4 %finish.1 = (bf16[4096,2,128]{2,1,0:T(2,128)(2,1)}, bf16[4096,2,128]{2,1,0:T(2,128)(2,1)}, bf16[1024,2048]{1,0:T(8,128)(2,1)}) custom-call(s32[1]{0:T(128)} %copy.14.pos_ref, bf16[4096,2,128]{2,1,0:T(2,128)(2,1)S(1)} %get-tuple-element.10.kc_buf, bf16[4096,2,128]{2,1,0:T(2,128)(2,1)S(1)} %get-tuple-element.11.vc_buf, ...), custom_call_target="tpu_custom_call" | custom-call | tf_op jit(solution)/shard_map/finish/pallas_call | solution.py:471
  (4 shorter events, 0.0 us)
